TPU v7x, 64 devices: a 2x2x8 block of a 4x4x8 slice. The times are simulated.
64 devices in a mesh: data: 4 (over x, y), stage: 16 (over z, core).
Axes of the slice: x: 2, y: 2, z: 8, core: 2. Of those that a mesh axis runs over, the one named last changes fastest.
The devices are a block of a 4x4x8 slice.
Arguments:
- x_rows: bfloat16 [16384, 576], P(('data', 'stage')), parts along dimension 0
- w_head: bfloat16 [49152, 576], P('stage')
- labels: int32 [16384], P('data'), parts along dimension 0
- loss_mask: int32 [16384], P('data'), parts along dimension 0
- w_embed: bfloat16 [49152, 576], P('stage')
- next_ids: int32 [16384], P('data'), parts along dimension 0
- stage_acts: bfloat16 [64, 4096, 576], P(('data', 'stage')), parts along dimension 0
- mlp_in: bfloat16 [16, 2, 576, 1536], P('stage')
- mlp_out: bfloat16 [16, 2, 1536, 576], P('stage')
Outputs:
- output 1: float32 [4], P('data'), parts along dimension 0
- output 2: float32 [16384, 576], P(('data', 'stage')), parts along dimension 0
- output 3: bfloat16 [196608, 576], P(('data', 'stage')), parts along dimension 0
- output 4: bfloat16 [16384, 576], P(('data', 'stage')), parts along dimension 0
- output 5: bfloat16 [64, 4096, 576], P(('data', 'stage')), parts along dimension 0
There are 4 independent parts. A program takes and returns all parts, laid end to end along the dimension named above; an argument that names none is the same for every part.
All inputs are finite; a program needn't handle non-finite values.
Results may differ from a plain program's by a relative error of at most 0.00125.
Values are sent between devices in bfloat16 or wider.
A program may use at most 768 MiB of HBM per device.

v0:
```python
import jax
import jax.numpy as jnp
from jax import lax
from jax.sharding import PartitionSpec as P


def mlp_layers(hidden, up_pair, down_pair):
    for layer_idx in range(up_pair.shape[0]):
        pre_act = jnp.dot(hidden, up_pair[layer_idx], preferred_element_type=jnp.float32)
        gelu_out = jax.nn.gelu(pre_act, approximate=True).astype(jnp.bfloat16)
        hidden = (hidden.astype(jnp.float32) + jnp.dot(gelu_out, down_pair[layer_idx], preferred_element_type=jnp.float32)).astype(jnp.bfloat16)
    return hidden


def solution(mesh):
    stages = mesh.shape['stage']
    row_spec = P(('data', 'stage'), None)
    vocab_spec = P('stage', None)
    layer_spec = P('stage', None, None, None)
    acts_spec = P(('data', 'stage'), None, None)

    def per_device(x_loc, w_loc, labels, loss_mask, e_loc, next_ids, acts_loc, up_loc, down_loc):
        stage_idx = lax.axis_index('stage')
        shard_rows = w_loc.shape[0]
        offset = stage_idx * shard_rows
        x_full = lax.all_gather(x_loc, 'stage', axis=0, tiled=True)
        logits = lax.dot_general(x_full, w_loc, (((1,), (1,)), ((), ())), preferred_element_type=jnp.float32)
        row_max = lax.pmax(jnp.max(logits, axis=1), 'stage')
        shifted = jnp.exp(logits - row_max[:, None])
        label_hit = jnp.arange(shard_rows, dtype=jnp.int32)[None, :] == (labels - offset)[:, None]
        local_stats = jnp.stack([jnp.sum(shifted, axis=1), jnp.sum(jnp.where(label_hit, logits, 0.0), axis=1)])
        row_stats = lax.psum(local_stats, 'stage')
        partition = row_stats[0]
        target_logit = row_stats[1]
        weight = loss_mask.astype(jnp.float32)
        token_count = jnp.maximum(jnp.sum(weight), 1.0)
        loss_value = jnp.sum(weight * (jnp.log(partition) + row_max - target_logit)) / token_count
        row_scale = weight / token_count
        grad_logits = ((shifted / partition[:, None] - label_hit.astype(jnp.float32)) * row_scale[:, None]).astype(jnp.bfloat16)
        grad_part = jnp.dot(grad_logits, w_loc, preferred_element_type=jnp.float32)
        grad_x = lax.psum_scatter(grad_part, 'stage', scatter_dimension=0, tiled=True)
        grad_head = lax.dot_general(grad_logits, x_full, (((0,), (0,)), ((), ())), preferred_element_type=jnp.float32).astype(jnp.bfloat16)
        local_ids = next_ids - offset
        in_shard = (local_ids >= 0) & (local_ids < shard_rows)
        picked = jnp.take(e_loc, jnp.clip(local_ids, 0, shard_rows - 1), axis=0)
        embed_part = jnp.where(in_shard[:, None], picked, jnp.zeros((), jnp.bfloat16))
        embed_rows = lax.psum_scatter(embed_part, 'stage', scatter_dimension=0, tiled=True)
        is_middle = (stage_idx > 0) & (stage_idx < stages - 1)
        stage_out = lax.cond(is_middle, lambda hidden: mlp_layers(hidden, up_loc[0], down_loc[0]), lambda hidden: hidden, acts_loc[0])
        return loss_value.reshape(1), grad_x, grad_head, embed_rows, stage_out[None]

    return jax.shard_map(
        per_device,
        mesh=mesh,
        in_specs=(row_spec, vocab_spec, P('data'), P('data'), vocab_spec, P('data'), acts_spec, layer_spec, layer_spec),
        out_specs=(P('data'), row_spec, row_spec, row_spec, acts_spec),
        check_vma=False,
    )
```

profile of v0, /device:TPU:21, one launch (start us, length us, event | category | flops | bytes accessed | tf_op | source)
XLA Modules:
  0.0 355.6 jit_solution(7566664022370922941)
XLA Ops:
  7.2 0.0 copy-start
  7.2 0.1 all-gather.2.cloned.1.call-start
  7.3 5.2 %copy.24 = bf16[1,4096,576]{1,2,0:T(8,128)(2,1)} copy(bf16[1,4096,576]{1,2,0:T(8,128)(2,1)} %param.17) | data formatting | bytes 9437184
  12.5 0.1 all-gather.2.cloned.1.call-update
  12.6 0.1 reduce-scatter.5.cloned.1.call-start
  12.6 6.1 %copy.16 = bf16[3072,576]{1,0:T(8,128)(2,1)} copy(bf16[3072,576]{0,1:T(8,128)(2,1)} %param.15) | data formatting | bytes 7077888 | tf_op args[4]
  18.7 0.7 fusion.34
  19.5 20.6 %gather_fusion = bf16[4096,576]{1,0:T(8,128)(2,1)} fusion(bf16[3072,576]{1,0:T(8,128)(2,1)} %copy.16, s32[4096]{0:T(1024)S(1)} %fusion.34), kind=kCustom, calls=%fused_computation | custom fusion | bytes 9453568 | tf_op jit(solution)/shard_map/jit(_take)/gather | solution.py:45
  40.1 0.0 copy-start.4
  40.1 0.7 compare_and_fusion.1
  40.9 6.0 %select_select_fusion = bf16[4096,576]{1,0:T(8,128)(2,1)} fusion(bf16[4096,576]{1,0:T(8,128)(2,1)} %gather_fusion, pred[4096]{0:T(1024)(128)(4,1)S(1)} %get-tuple-element.44, pred[4096]{0:T(1024)(128)(4,1)S(1)} %get-tuple-element.43), kind=kLoop, calls=%fused_computation.41 | loop fusion | flops 4718592 | bytes 9445376 | tf_op jit(solution)/shard_map/jit(_where)/select_n | solution.py:46
  46.9 0.1 reduce-scatter.5.cloned.1.call-update
  46.9 0.1 reduce-scatter.3.cloned.1.call-start
  47.0 0.0 copy-done.4
  47.0 0.6 broadcast_subtract_fusion
  47.6 17.5 %all-gather.2.cloned.1.call-done = bf16[4096,576]{0,1:T(8,128)(2,1)} async-done(((bf16[256,576]{0,1:T(8,128)(2,1)}), bf16[4096,576]{0,1:T(8,128)(2,1)}) %all-gather.2.cloned.1.call-update) | async-done | bytes 4718608 | tf_op jit(solution)/shard_map/all_gather | solution.py:26
  65.1 0.0 copy-done
  65.1 27.2 %fusion.36 = (f32[4096]{0:T(1024)}, f32[4096,3072]{0,1:T(8,128)}) fusion(bf16[4096,576]{0,1:T(8,128)(2,1)} %all-gather.2.cloned.1.call-done, bf16[3072,576]{0,1:T(8,128)(2,1)S(1)} %copy-done), kind=kOutput, calls=%fused_computation.53 | convolution fusion | flops 14508093440 | bytes 58605568 | tf_op jit(solution)/shard_map/dot_general | solution.py:27
  92.3 45.2 %pmax.7 = f32[4096]{0:T(1024)S(1)} all-reduce(f32[4096]{0:T(1024)} %get-tuple-element.45), channel_id=1, replica_groups=mesh['data'=4,'stage'=16] {'stage'}, use_global_device_ids=true, to_apply=%region_1.0 | all-reduce | flops 4096 | bytes 32768 | tf_op jit(solution)/shard_map/pmax | solution.py:28
  137.5 22.2 %fusion.33 = (f32[4096]{0:T(1024)S(1)}, f32[4096]{0:T(1024)S(1)}) fusion(f32[4096,3072]{0,1:T(8,128)} %get-tuple-element.46, f32[4096]{0:T(1024)S(1)} %pmax.7, s32[4096]{0:T(1024)} %broadcast_subtract_fusion), kind=kLoop, calls=%fused_computation.40 | loop fusion | flops 62906368 | bytes 50397184 | tf_op jit(solution)/shard_map/reduce_sum | solution.py:31
  159.7 0.6 pad_maximum_fusion
  160.3 46.3 %psum.7 = f32[2,4096]{1,0:T(2,128)} all-reduce(f32[2,4096]{1,0:T(2,128)} %pad_maximum_fusion), channel_id=1, replica_groups=mesh['data'=4,'stage'=16] {'stage'}, use_global_device_ids=true, to_apply=%region_4.5 | all-reduce | flops 8192 | bytes 65536 | tf_op jit(solution)/shard_map/psum | solution.py:32
  206.6 0.9 fusion.35
  207.5 0.0 copy-start.3
  207.5 0.6 copy-done.3
  208.1 1.4 convert_reduce_fusion
  210.2 1.3 convert_divide_fusion
  211.5 31.2 %multiply_convert_fusion = bf16[4096,3072]{0,1:T(8,128)(2,1)} fusion(f32[4096,3072]{0,1:T(8,128)} %get-tuple-element.46, f32[4096]{0:T(1024)} %convert_divide_fusion, f32[4096]{0:T(1024)} %bitcast.35, s32[4096]{0:T(1024)} %broadcast_subtract_fusion, f32[4096]{0:T(1024)S(1)} %pmax.7), kind=kLoop, calls=%fused_computation.36 | loop fusion | flops 88080384 | bytes 75563008 | tf_op jit(solution)/shard_map/convert_element_type | solution.py:39
  242.7 21.7 %fusion.37 = f32[4096,576]{0,1:T(8,128)} fusion(bf16[3072,576]{0,1:T(8,128)(2,1)S(1)} %copy-done, bf16[4096,3072]{0,1:T(8,128)(2,1)} %multiply_convert_fusion), kind=kOutput, calls=%fused_computation.54 | convolution fusion | flops 14495514624 | bytes 38141952 | tf_op jit(solution)/shard_map/dot_general | solution.py:40
  264.4 0.0 copy-start.2
  264.4 0.1 reduce-scatter.3.cloned.1.call-update
  264.4 1.9 copy-done.2
  266.4 57.4 %conditional.1 = (bf16[1,4096,576]{1,2,0:T(8,128)(2,1)}) conditional(s32[]{:T(128)} %convert_element_type.37, bf16[4096,576]{0,1:T(8,128)(2,1)} %bitcast.31, (bf16[4096,576]{0,1:T(8,128)(2,1)}, bf16[1,2,576,1536]{3,2,1,0:T(8,128)(2,1)}, bf16[1,2,1536,576]{2,3,1,0:T(8,128)(2,1)S(1)}) %tuple.45), branch_computations={%region_9.10_spmd, %region_10.11_spmd} | conditional | flops 29118431232 | bytes 57016356 | solution.py:49
  266.6 3.9 %copy.17 = bf16[1,2,1536,576]{3,2,1,0:T(8,128)(2,1)} copy(bf16[1,2,1536,576]{2,3,1,0:T(8,128)(2,1)S(1)} %get-tuple-element.31) | data formatting | bytes 7077888 | tf_op jit(solution)/shard_map
  270.4 0.0 copy-start.5
  270.4 26.7 %add_convert_fusion.1 = bf16[4096,576]{0,1:T(8,128)(2,1)} fusion(bf16[4096,576]{0,1:T(8,128)(2,1)} %get-tuple-element.16, bf16[1,2,1536,576]{3,2,1,0:T(8,128)(2,1)} %copy.17, bf16[1,2,576,1536]{3,2,1,0:T(8,128)(2,1)} %get-tuple-element.27), kind=kOutput, calls=%fused_computation.20 | convolution fusion | flops 14559215616 | bytes 17891328 | tf_op jit(solution)/shard_map/cond/branch_1_fun/dot_general | solution.py:11
  297.1 0.0 copy-done.5
  297.1 26.3 %fusion.16 = bf16[1,4096,576]{1,2,0:T(8,128)(2,1)} fusion(bf16[4096,576]{0,1:T(8,128)(2,1)} %add_convert_fusion.1, bf16[1,2,1536,576]{3,2,1,0:T(8,128)(2,1)} %copy.17, bf16[1,2,576,1536]{3,2,1,0:T(8,128)(2,1)S(1)} %copy-done.5), kind=kOutput, calls=%fused_computation.21 | convolution fusion | flops 14559215616 | bytes 17891328 | tf_op jit(solution)/shard_map/cond/branch_1_fun/dot_general | solution.py:11
  324.4 0.0 copy-start.1
  324.5 21.1 %convolution_convert_fusion = bf16[3072,576]{0,1:T(8,128)(2,1)} fusion(bf16[4096,3072]{0,1:T(8,128)(2,1)} %multiply_convert_fusion, bf16[4096,576]{0,1:T(8,128)(2,1)} %all-gather.2.cloned.1.call-done), kind=kOutput, calls=%fused_computation.42 | convolution fusion | flops 14497284096 | bytes 33423360 | tf_op jit(solution)/shard_map/dot_general | solution.py:42
  345.6 0.0 reduce-scatter.5.cloned.1.call-done
  345.6 1.8 copy.18
  347.4 0.0 reduce-scatter.3.cloned.1.call-done
  347.4 0.0 copy-done.1
Async XLA Ops:
  7.2 57.9 %copy-start = (bf16[3072,576]{0,1:T(8,128)(2,1)S(1)}, bf16[3072,576]{0,1:T(8,128)(2,1)}, u32[]{:S(2)}) copy-start(bf16[3072,576]{0,1:T(8,128)(2,1)} %param.12) | copy-start | bytes 10616836
  7.2 57.9 %all-gather.2.cloned.1.call-start = ((), (), s32[]{:S(2)}) async-start(), calls=%async_computation.2 | async-start | bytes 5013504 | tf_op jit(solution)/shard_map/all_gather | solution.py:26
  12.6 333.0 %reduce-scatter.5.cloned.1.call-start = ((), (), s32[]{:S(2)}) async-start(), calls=%async_computation.4 | async-start | bytes 5570560 | tf_op jit(solution)/shard_map/reduce_scatter | solution.py:47
  40.1 6.9 %copy-start.4 = (s32[4096]{0:T(1024)S(1)}, s32[4096]{0:T(1024)}, u32[]{:S(2)}) copy-start(s32[4096]{0:T(1024)} %param.13) | copy-start | bytes 49156
  46.9 300.5 %reduce-scatter.3.cloned.1.call-start = ((), (), s32[]{:S(2)}) async-start(), calls=%async_computation.3 | async-start | bytes 10027008 | tf_op jit(solution)/shard_map/reduce_scatter | solution.py:41
  207.5 0.6 copy-start.3
  264.4 2.0 copy-start.2
  270.4 26.7 %copy-start.5 = (bf16[1,2,576,1536]{3,2,1,0:T(8,128)(2,1)S(1)}, bf16[1,2,576,1536]{3,2,1,0:T(8,128)(2,1)}, u32[]{:S(2)}) copy-start(bf16[1,2,576,1536]{3,2,1,0:T(8,128)(2,1)} %get-tuple-element.27) | copy-start | bytes 10616836 | tf_op jit(solution)/shard_map/cond
  324.4 23.0 %copy-start.1 = (bf16[3072,576]{0,1:T(8,128)(2,1)S(1)}, bf16[3072,576]{0,1:T(8,128)(2,1)}, u32[]{:S(2)}) copy-start(bf16[3072,576]{0,1:T(8,128)(2,1)} %param.12) | copy-start | bytes 10616836
Sparse Core Ops, SparseCore 0:
  12.7 52.3 all-gather.1
  67.4 57.4 reduce-scatter.4
  264.5 68.9 reduce-scatter.2
where the time goes:
time: 362 us; the launch traced here: 356 us
  matrix products  123 us (34%)
  blocking collectives  91.5 us (25%)
  other arithmetic  64.9 us (18%)
  local copies, waits for them, and re-layouts  41.1 us (11%)
  waiting for transfers between devices  17.6 us (5%)
  between operations  16.8 us (5%)
    dot_general x2, matrix products, mlp_layers(): jnp.dot(gelu_out, down_pair[layer_idx], preferred_element_type=jnp.float32)  53 us
    psum x1, blocking collectives, per_device(): row_stats = lax.psum(local_stats, 'stage')  46.3 us
    pmax x1, blocking collectives, per_device(): row_max = lax.pmax(jnp.max(logits, axis=1), 'stage')  45.2 us
    convert_element_type x1, other arithmetic, per_device(): ((shifted / partition[:, None] - label_hit.astype(jnp.float32)) * row_sca...  31.2 us
    dot_general x1, matrix products, per_device(): lax.dot_general(x_full, w_loc, (((1,), (1,)), ((), ())), preferred_elemen...  27.2 us
    reduce_sum x1, other arithmetic, per_device(): jnp.sum(shifted, axis=1)  22.2 us
    dot_general x1, matrix products, per_device(): grad_part = jnp.dot(grad_logits, w_loc, preferred_element_type=jnp.float32)  21.7 us
    dot_general x1, matrix products, per_device(): lax.dot_general(grad_logits, x_full, (((0,), (0,)), ((), ())), preferred_...  21.1 us
  transfers between devices with their start and end apart: 3, of which 1 were waited for; matrix products, arithmetic and copies ran while one was open for 62% of the time, Pallas kernels for 0%

commit v1 on v0

v1 whole, which is shorter than its diff:
```python
import functools

import jax
import jax.numpy as jnp
from jax import lax
from jax.experimental import pallas as pl
from jax.experimental.pallas import tpu as pltpu
from jax.sharding import PartitionSpec as P

F32 = jnp.float32
BF16 = jnp.bfloat16
MESH = pl.DeviceIdType.MESH
CHUNK = 512
GROUP = 2
MIB = 1024 * 1024


def mm(a, b, ca, cb):
    return lax.dot_general(a, b, (((ca,), (cb,)), ((), ())), preferred_element_type=F32)


def params(limit, **kw):
    return pltpu.CompilerParams(vmem_limit_bytes=limit * MIB, **kw)


def cost(flops, nbytes):
    return pl.CostEstimate(flops=int(flops), bytes_accessed=int(nbytes), transcendentals=0)


def transpose_into(dst_ref, src, step):
    for c in range(0, src.shape[1], step):
        dst_ref[pl.ds(c, step), :] = src[:, c:c + step].T


def side_by_side(ref):
    return jnp.concatenate([ref[b] for b in range(ref.shape[0])], axis=1)


def gelu(x):
    k = 0.7978845608028654
    inner = x * (k + (k * 0.044715) * (x * x))
    half = 0.5 * x
    return half + half * jnp.tanh(inner)


def mlp_kernel(a_ref, up_ref, down_ref, y_ref, upt_ref):
    layers = up_ref.shape[0]
    stage = lax.axis_index('stage')
    middle = (stage > 0) & (stage < lax.axis_size('stage') - 1)

    @pl.when(pl.program_id(0) == 0)
    def _():
        for i in range(layers):
            transpose_into(upt_ref.at[i], up_ref[i], 256)

    @pl.when(middle)
    def _():
        h = a_ref[...]
        for i in range(layers):
            u = jnp.concatenate(
                [gelu(mm(upt_ref[i, pl.ds(c, 512), :], h, 1, 0)).astype(BF16) for c in range(0, up_ref.shape[2], 512)], axis=0)
            h = (h.astype(F32) + mm(down_ref[i], u, 1, 0)).astype(BF16)
        y_ref[...] = h

    @pl.when(jnp.logical_not(middle))
    def _():
        y_ref[...] = a_ref[...]


def mlp(at, up, down):
    dim, tokens = at.shape
    layers, _, hidden = up.shape
    tile = 512
    return pl.pallas_call(
        mlp_kernel,
        grid=(tokens // tile,),
        in_specs=[
            pl.BlockSpec((dim, tile), lambda i: (0, i)),
            pl.BlockSpec((layers, dim, hidden), lambda i: (0, 0, 0)),
            pl.BlockSpec((layers, dim, hidden), lambda i: (0, 0, 0)),
        ],
        out_specs=pl.BlockSpec((dim, tile), lambda i: (0, i)),
        out_shape=jax.ShapeDtypeStruct((dim, tokens), BF16),
        scratch_shapes=[pltpu.VMEM((layers, hidden, dim), BF16)],
        compiler_params=params(48),
        cost_estimate=cost(4 * layers * tokens * dim * hidden, 4 * tokens * dim + 4 * layers * dim * hidden),
        name='mlp',
    )(at, up, down)


def embed_kernel(ids_ref, et_ref, out_ref):
    rows = et_ref.shape[1]
    tok = ids_ref.shape[2]
    index = lax.broadcasted_iota(jnp.int32, (rows, GROUP * tok), 0)
    hot = jnp.where(index == side_by_side(ids_ref), 1.0, 0.0).astype(BF16)
    out = mm(et_ref[...], hot, 1, 0).astype(BF16)
    for b in range(GROUP):
        out_ref[b] = out[:, b * tok:(b + 1) * tok]


def embed(ids, et):
    n, _, tok = ids.shape
    dim, rows = et.shape
    return pl.pallas_call(
        embed_kernel,
        grid=(n // GROUP,),
        in_specs=[
            pl.BlockSpec((GROUP, 1, tok), lambda i: (i, 0, 0)),
            pl.BlockSpec((dim, rows), lambda i: (0, 0)),
        ],
        out_specs=pl.BlockSpec((GROUP, dim, tok), lambda i: (i, 0, 0)),
        out_shape=jax.ShapeDtypeStruct((n, dim, tok), BF16),
        compiler_params=params(48),
        cost_estimate=cost(2 * n * tok * dim * rows, 2 * dim * (n * tok + rows)),
        name='embed',
    )(ids, et)


def logits_kernel(wt_ref, x_ref, lab_ref, e_ref, cm_ref, st_ref, w_ref):
    rows = wt_ref.shape[1]
    tok = x_ref.shape[2]

    @pl.when(pl.program_id(0) == 0)
    def _():
        transpose_into(w_ref, wt_ref, 256)

    x = side_by_side(x_ref)
    lab = side_by_side(lab_ref)
    index = lax.broadcasted_iota(jnp.int32, (CHUNK, GROUP * tok), 0)
    maxes, sums = [], []
    target = jnp.zeros((1, GROUP * tok), F32)
    for c in range(rows // CHUNK):
        sl = pl.ds(c * CHUNK, CHUNK)
        z = mm(w_ref[sl, :], x, 1, 0)
        m = jnp.max(z, axis=0, keepdims=True)
        e = jnp.exp(z - m)
        for b in range(GROUP):
            e_ref[b, sl, :] = e[:, b * tok:(b + 1) * tok]
        maxes.append(m)
        sums.append(jnp.sum(e, axis=0, keepdims=True))
        target += jnp.sum(jnp.where(index == lab - c * CHUNK, z, 0.0), axis=0, keepdims=True)
    m = functools.reduce(jnp.maximum, maxes)
    s = sum(si * jnp.exp(mi - m) for mi, si in zip(maxes, sums))
    cm = jnp.concatenate(maxes + [jnp.zeros((8 - len(maxes), GROUP * tok), F32)], axis=0)
    st = jnp.concatenate([m, s, target, jnp.zeros((5, GROUP * tok), F32)], axis=0)
    for b in range(GROUP):
        cm_ref[b] = cm[:, b * tok:(b + 1) * tok]
        st_ref[b] = st[:, b * tok:(b + 1) * tok]


def logits(wt, x, lab):
    dim, rows = wt.shape
    n, _, tok = x.shape
    block = lambda r, c: pl.BlockSpec((GROUP, r, c), lambda i: (i, 0, 0))
    return pl.pallas_call(
        logits_kernel,
        grid=(n // GROUP,),
        in_specs=[pl.BlockSpec((dim, rows), lambda i: (0, 0)), block(dim, tok), block(1, tok)],
        out_specs=[block(rows, tok), block(8, tok), block(8, tok)],
        out_shape=[
            jax.ShapeDtypeStruct((n, rows, tok), F32),
            jax.ShapeDtypeStruct((n, 8, tok), F32),
            jax.ShapeDtypeStruct((n, 8, tok), F32),
        ],
        scratch_shapes=[pltpu.VMEM((rows, dim), BF16)],
        compiler_params=params(56),
        cost_estimate=cost(2 * n * tok * dim * rows, 4 * n * tok * rows),
        name='logits',
    )(wt, x, lab)


def stats_kernel(n, st_ref, mask_ref, out_ref, loss_ref, got, every, send1, recv1, send2, recv2):
    me = lax.axis_index('stage')
    barrier = pltpu.get_barrier_semaphore()
    peers = [lax.rem(me + d, n) for d in range(n)]
    for d in range(1, n):
        pl.semaphore_signal(barrier, inc=1, device_id={'stage': peers[d]}, device_id_type=MESH)
    pl.semaphore_wait(barrier, n - 1)

    first = []
    for d in range(1, n):
        first.append(pltpu.make_async_remote_copy(
            src_ref=st_ref.at[peers[d]], dst_ref=got.at[d], send_sem=send1.at[d], recv_sem=recv1.at[d],
            device_id={'stage': peers[d]}, device_id_type=MESH))
        first[-1].start()
    weight = mask_ref[...]
    count = jnp.maximum(jnp.sum(weight, keepdims=True)[0], 1.0)
    for copy in first:
        copy.wait()
    parts = [st_ref[me]] + [got[d] for d in range(1, n)]
    m = functools.reduce(jnp.maximum, [p[0:1] for p in parts])
    total = sum(p[1:2] * jnp.exp(p[0:1] - m) for p in parts)
    target = sum(p[2:3] for p in parts)
    w = mask_ref[me]
    scale = w / count
    term = w * (jnp.log(total) + m - target)
    mine = jnp.concatenate([m, scale / total, scale, term, jnp.zeros((4, m.shape[1]), F32)], axis=0)
    every[me] = mine
    second = []
    for d in range(1, n):
        second.append(pltpu.make_async_remote_copy(
            src_ref=every.at[me], dst_ref=every.at[me], send_sem=send2.at[d], recv_sem=recv2.at[d],
            device_id={'stage': peers[d]}, device_id_type=MESH))
        second[-1].start()
    for copy in second:
        copy.wait()
    out_ref[...] = every[...]
    loss_ref[...] = jnp.broadcast_to(jnp.sum(every[:, 3, :], keepdims=True) / count, loss_ref.shape)


def stats(st, mask):
    n, _, tok = st.shape
    vmem = pl.BlockSpec(memory_space=pltpu.VMEM)
    return pl.pallas_call(
        functools.partial(stats_kernel, n),
        in_specs=[vmem, vmem],
        out_specs=[vmem, vmem],
        out_shape=[jax.ShapeDtypeStruct((n, 8, tok), F32), jax.ShapeDtypeStruct((8, 128), F32)],
        scratch_shapes=[
            pltpu.VMEM((n, 8, tok), F32),
            pltpu.VMEM((n, 8, tok), F32),
        ] + [pltpu.SemaphoreType.DMA((n,))] * 4,
        compiler_params=params(16, collective_id=0, has_side_effects=True),
        cost_estimate=cost(1e9, 2e6),
        name='stats',
    )(st, mask)


def grad_kernel(wt_ref, e_ref, cm_ref, gs_ref, lab_ref, g_ref, dx_ref):
    rows = wt_ref.shape[1]
    tok = e_ref.shape[2]
    index = lax.broadcasted_iota(jnp.int32, (CHUNK, tok), 0)
    for b in range(GROUP):
        m, over, scale = gs_ref[b, 0:1, :], gs_ref[b, 1:2, :], gs_ref[b, 2:3, :]
        for c in range(rows // CHUNK):
            sl = pl.ds(c * CHUNK, CHUNK)
            p = e_ref[b, sl, :] * (jnp.exp(cm_ref[b, c:c + 1, :] - m) * over)
            hit = index == lab_ref[b] - c * CHUNK
            g_ref[b, sl, :] = jnp.where(hit, p - scale, p).astype(BF16)
    dx = mm(wt_ref[...], side_by_side(g_ref), 1, 0)
    for b in range(GROUP):
        dx_ref[b] = dx[:, b * tok:(b + 1) * tok]


def grad(wt, e, cm, gs, lab):
    dim, rows = wt.shape
    n, _, tok = e.shape
    block = lambda r, c: pl.BlockSpec((GROUP, r, c), lambda i: (i, 0, 0))
    return pl.pallas_call(
        grad_kernel,
        grid=(n // GROUP,),
        in_specs=[pl.BlockSpec((dim, rows), lambda i: (0, 0)), block(rows, tok), block(8, tok), block(8, tok), block(1, tok)],
        out_specs=[block(rows, tok), block(dim, tok)],
        out_shape=[jax.ShapeDtypeStruct((n, rows, tok), BF16), jax.ShapeDtypeStruct((n, dim, tok), F32)],
        compiler_params=params(56),
        cost_estimate=cost(2 * n * tok * dim * rows, 6 * n * tok * rows),
        name='grad',
    )(wt, e, cm, gs, lab)


def head_kernel(x_ref, g_ref, out_ref):
    out_ref[...] = mm(side_by_side(x_ref), side_by_side(g_ref), 1, 1).astype(BF16)


def head(x, g):
    n, dim, tok = x.shape
    rows = g.shape[1]
    tile = 512
    return pl.pallas_call(
        head_kernel,
        grid=(rows // tile,),
        in_specs=[pl.BlockSpec((n, dim, tok), lambda i: (0, 0, 0)), pl.BlockSpec((n, tile, tok), lambda i: (0, i, 0))],
        out_specs=pl.BlockSpec((dim, tile), lambda i: (0, i)),
        out_shape=jax.ShapeDtypeStruct((dim, rows), BF16),
        compiler_params=params(56),
        cost_estimate=cost(2 * n * tok * dim * rows, 2 * n * tok * rows),
        name='head',
    )(x, g)


def solution(mesh):
    n = mesh.shape['stage']
    row_spec = P(('data', 'stage'), None)
    vocab_spec = P('stage', None)
    layer_spec = P('stage', None, None, None)
    acts_spec = P(('data', 'stage'), None, None)

    def per_device(x_loc, w_loc, labels, loss_mask, e_loc, next_ids, acts_loc, up_loc, down_loc):
        tok = x_loc.shape[0]
        offset = lax.axis_index('stage') * w_loc.shape[0]
        wt = w_loc.T
        x = lax.all_gather(x_loc.T, 'stage', axis=0)
        ids = (next_ids - offset).reshape(n, 1, tok)
        lab = (labels - offset).reshape(n, 1, tok)
        mask = loss_mask.astype(F32).reshape(n, 1, tok)
        embed_part = embed(ids, e_loc.T)
        embed_rows = lax.psum_scatter(embed_part, 'stage', scatter_dimension=0)
        stage_out = mlp(acts_loc[0].T, up_loc[0], jnp.swapaxes(down_loc[0], 1, 2))
        e, cm, st = logits(wt, x, lab)
        gs, loss = stats(st, mask)
        g, dx_part = grad(wt, e, cm, gs, lab)
        dx = lax.psum_scatter(dx_part, 'stage', scatter_dimension=0)
        dw = head(x, g)
        return loss[0, :1], dx.T, dw.T, embed_rows.T, stage_out.T[None]

    return jax.shard_map(
        per_device,
        mesh=mesh,
        in_specs=(row_spec, vocab_spec, P('data'), P('data'), vocab_spec, P('data'), acts_spec, layer_spec, layer_spec),
        out_specs=(P('data'), row_spec, row_spec, row_spec, acts_spec),
        check_vma=False,
    )
```

time: 362 us -> 214 us (0.59); the launches traced: 356 us -> 212 us
  Pallas kernels: 0 us -> 163 us
  matrix products: 123 us -> 0 us
  blocking collectives: 91.5 us -> 0 us
  other arithmetic: 64.9 us -> 1.33 us
  local copies, waits for them, and re-layouts: 41.1 us -> 6.6 us
  waiting for transfers between devices: 17.6 us -> 27.1 us
    pallas_call x0 -> x6, Pallas kernels: none -> 163 us  [the longest x1 41 us: mlp(): pl.pallas_call(mlp_kernel, grid=(tokens // tile,), in_specs=[pl.BlockSpec...]
    dot_general x5 -> x0, matrix products: 123 us -> none  [the longest x2 53 us: mlp_layers(): jnp.dot(gelu_out, down_pair[layer_idx], preferred_element_type=jnp.float32)]
    psum x1 -> x0, blocking collectives: 46.3 us -> none  [per_device(): row_stats = lax.psum(local_stats, 'stage')]
    pmax x1 -> x0, blocking collectives: 45.2 us -> none  [per_device(): row_max = lax.pmax(jnp.max(logits, axis=1), 'stage')]
    convert_element_type x1, other arithmetic: 31.2 us -> 0.01 us  [per_device(): mask = loss_mask.astype(F32).reshape(n, 1, tok)]
    reduce_sum x2 -> x0, other arithmetic: 23.6 us -> none  [the longest x1 22.2 us: per_device(): jnp.sum(shifted, axis=1)]
    gather x1 -> x0, local copies, waits for them, and re-layouts: 20.6 us -> none  [per_device(): picked = jnp.take(e_loc, jnp.clip(local_ids, 0, shard_rows - 1), axis=0)]
    unnamed x13 -> x12, local copies, waits for them, and re-layouts: 15.7 us -> 6.09 us
  transfers between devices with their start and end apart: 3 -> 3, of which waited for: 1 -> 2; matrix products, arithmetic and copies ran while one was open for 62% -> 1% of each run, Pallas kernels for 0% -> 77%
where the time goes in v1:
time: 214 us; the launch traced here: 212 us
  Pallas kernels  163 us (76%)
  waiting for transfers between devices  27.1 us (13%)
  between operations  13.8 us (6%)
  local copies, waits for them, and re-layouts  6.6 us (3%)
    pallas_call x1, Pallas kernels, mlp(): pl.pallas_call(mlp_kernel, grid=(tokens // tile,), in_specs=[pl.BlockSpec...  41 us
    pallas_call x1, Pallas kernels, logits(): pl.pallas_call(logits_kernel, grid=(n // GROUP,), in_specs=[pl.BlockSpec(...  35.2 us
    pallas_call x1, Pallas kernels, grad(): pl.pallas_call(grad_kernel, grid=(n // GROUP,), in_specs=[pl.BlockSpec((d...  32.6 us
    all_gather x1, waiting for transfers between devices, per_device(): x = lax.all_gather(x_loc.T, 'stage', axis=0)  24.7 us
    pallas_call x1, Pallas kernels, head(): pl.pallas_call(head_kernel, grid=(rows // tile,), in_specs=[pl.BlockSpec(...  20.3 us
    pallas_call x1, Pallas kernels, stats(): pl.pallas_call(functools.partial(stats_kernel, n), in_specs=[vmem, vmem],...  17 us
    pallas_call x1, Pallas kernels, embed(): pl.pallas_call(embed_kernel, grid=(n // GROUP,), in_specs=[pl.BlockSpec((...  16.9 us
    unnamed x12, local copies, waits for them, and re-layouts  6.09 us
  transfers between devices with their start and end apart: 3, of which 2 were waited for; matrix products, arithmetic and copies ran while one was open for 1% of the time, Pallas kernels for 77%

profile of v1, /device:TPU:21, one launch (start us, length us, event | category | flops | bytes accessed | tf_op | source)
XLA Modules:
  0.0 212.2 jit_solution(6935087644897550316)
XLA Ops:
  7.2 0.1 all-gather.3.cloned.1.call-start
  7.2 0.7 all-gather.3.cloned.1.call-update
  8.0 0.1 reduce-scatter.5.cloned.1.call-start
  8.0 0.7 broadcast_subtract_fusion
  8.8 0.0 copy-start.1
  8.8 2.0 copy-done.1
  10.8 16.9 %embed.1 = bf16[16,576,256]{2,1,0:T(8,128)(2,1)} custom-call(s32[16,1,256]{2,1,0:T(1,128)S(1)} %bitcast.26, bf16[576,3072]{1,0:T(8,128)(2,1)S(1)} %bitcast.27), custom_call_target="tpu_custom_call" | custom-call | flops 14495514624 | bytes 8257536 | tf_op jit(solution)/shard_map/embed/pallas_call | solution.py:104
  27.7 0.0 copy-start.4
  27.7 0.0 copy-start.5
  27.7 0.1 reduce-scatter.5.cloned.1.call-update
  27.8 0.1 reduce-scatter.3.cloned.1.call-start
  27.8 0.6 copy-done.4
  28.4 0.0 copy-done.5
  28.4 0.6 broadcast_subtract_fusion.1
  29.0 24.7 %all-gather.3.cloned.1.call-done = bf16[9216,256]{1,0:T(8,128)(2,1)} async-done(((bf16[576,256]{1,0:T(8,128)(2,1)}), bf16[9216,256]{1,0:T(8,128)(2,1)}) %all-gather.3.cloned.1.call-update) | async-done | bytes 4718608 | tf_op jit(solution)/shard_map/all_gather | solution.py:292
  53.7 35.2 %logits.1 = (f32[16,3072,256]{2,1,0:T(8,128)}, f32[16,8,256]{2,1,0:T(8,128)}, f32[16,8,256]{2,1,0:T(8,128)}) custom-call(bf16[576,3072]{1,0:T(8,128)(2,1)} %bitcast.29, bf16[16,576,256]{2,1,0:T(8,128)(2,1)} %bitcast.35, s32[16,1,256]{2,1,0:T(1,128)} %bitcast.32), custom_call_target="tpu_custom_call" | custom-call | flops 14495514624 | bytes 50331648 | tf_op jit(solution)/shard_map/logits/pallas_call | solution.py:155
  88.9 0.0 copy-start.3
  88.9 0.9 copy-done.3
  89.8 17.0 %stats.1 = (f32[16,8,256]{2,1,0:T(8,128)S(1)}, f32[8,128]{1,0:T(8,128)S(1)}) custom-call(f32[16,8,256]{2,1,0:T(8,128)S(1)} %copy-done.3, f32[16,1,256]{2,1,0:T(1,128)S(1)} %bitcast.25), custom_call_target="tpu_custom_call" | custom-call | flops 1000000000 | bytes 2000000 | tf_op jit(solution)/shard_map/stats/pallas_call | solution.py:214
  106.8 0.0 copy-start
  106.8 0.6 copy-done
  107.5 32.6 %grad.1 = (bf16[16,3072,256]{2,1,0:T(8,128)(2,1)}, f32[16,576,256]{2,1,0:T(8,128)}) custom-call(bf16[576,3072]{1,0:T(8,128)(2,1)} %bitcast.30, f32[16,3072,256]{2,1,0:T(8,128)} %get-tuple-element.14.e_ref, f32[16,8,256]{2,1,0:T(8,128)} %get-tuple-element.15.cm_ref, f32[16,8,256]{2,1,0:T(8,128)} %copy-done, s32[16,1,256]{2,1,0:T(1,128)} %bitcast.33), custom_call_target="tpu_custom_call" | custom-call | flops 14495514624 | bytes 75497472 | tf_op jit(solution)/shard_map/grad/pallas_call | solution.py:249
  140.1 0.0 copy-start.2
  140.1 0.1 reduce-scatter.3.cloned.1.call-update
  140.2 1.9 copy-done.2
  142.1 41.0 %mlp.1 = bf16[576,4096]{1,0:T(8,128)(2,1)} custom-call(bf16[576,4096]{1,0:T(8,128)(2,1)} %bitcast.34, bf16[2,576,1536]{2,1,0:T(8,128)(2,1)S(1)} %bitcast.28, bf16[2,576,1536]{2,1,0:T(8,128)(2,1)} %bitcast.37), custom_call_target="tpu_custom_call" | custom-call | flops 28991029248 | bytes 16515072 | tf_op jit(solution)/shard_map/mlp/pallas_call | solution.py:74
  183.2 0.5 slice.3
  183.7 20.3 %head.1 = bf16[576,3072]{1,0:T(8,128)(2,1)} custom-call(bf16[16,576,256]{2,1,0:T(8,128)(2,1)} %bitcast.36, bf16[16,3072,256]{2,1,0:T(8,128)(2,1)} %get-tuple-element.18.g_ref), custom_call_target="tpu_custom_call" | custom-call | flops 14495514624 | bytes 25165824 | tf_op jit(solution)/shard_map/head/pallas_call | solution.py:269
  204.0 0.0 reduce-scatter.5.cloned.1.call-done
  204.0 1.6 reduce-scatter.3.cloned.1.call-done
  (1 shorter events, 0.0 us)
Async XLA Ops:
  7.2 46.5 %all-gather.3.cloned.1.call-start = ((), (), s32[]{:S(2)}) async-start(), calls=%async_computation.4 | async-start | bytes 5013504 | tf_op jit(solution)/shard_map/all_gather | solution.py:292
  8.0 196.0 %reduce-scatter.5.cloned.1.call-start = ((), (), s32[]{:S(2)}) async-start(), calls=%async_computation.3 | async-start | bytes 5013504 | tf_op jit(solution)/shard_map/reduce_scatter | solution.py:297
  8.8 2.0 copy-start.1
  27.7 0.7 copy-start.4
  27.7 0.7 copy-start.5
  27.8 177.9 %reduce-scatter.3.cloned.1.call-start = ((), (), s32[]{:S(2)}) async-start(), calls=%async_computation.2 | async-start | bytes 10027008 | tf_op jit(solution)/shard_map/reduce_scatter | solution.py:302
  88.9 0.9 copy-start.3
  106.8 0.7 copy-start
  140.1 2.0 copy-start.2
Sparse Core Ops, SparseCore 0:
  9.6 44.0 all-gather.2
  56.7 61.1 reduce-scatter.4
  140.3 65.2 reduce-scatter.2

commit v2 on v1

--- a/solution.py
+++ b/solution.py
@@ -226,56 +226,199 @@
     )(st, mask)
 
 
-def grad_kernel(wt_ref, e_ref, cm_ref, gs_ref, lab_ref, g_ref, dx_ref):
-    rows = wt_ref.shape[1]
-    tok = e_ref.shape[2]
+def grad_kernel(n, e_hbm, w_hbm, x_hbm, cm_ref, gs_ref, lab_ref, dx_ref, dw_ref, w_buf, x_buf, e_buf, g_buf, send_buf, own, pair,
+                chain, load_sem, e_sem, pair_send, pair_recv, chain_send, chain_recv):
+    stage = lax.axis_index('stage')
+    chips = n // 2
+    far = chips // 2
+    z, core = stage // 2, lax.rem(stage, 2)
+    dim, tok = dx_ref.shape
+    rows = w_buf.shape[1]
+    half = dim // 2
+    partner = {'stage': 2 * z + 1 - core}
+    ahead = {'stage': 2 * lax.rem(z + 1, chips) + core}
+    behind = {'stage': 2 * lax.rem(z + chips - 1, chips) + core}
+
+    def chip_at(i):
+        size = far - (i + 1) // 2
+        sign = 2 * lax.rem(i, 2) - 1
+        return lax.rem(z + sign * size + chips, chips)
+
+    def block_at(i, own_side):
+        return 2 * chip_at(i) + (core if own_side else 1 - core)
+
+    def load_e(i, slot):
+        return pltpu.make_async_copy(e_hbm.at[block_at(i, slot == 1)], e_buf.at[slot], e_sem.at[slot])
+
+    for slot in range(2):
+        load_e(0, slot).start()
+    load_w = pltpu.make_async_copy(w_hbm, w_buf, load_sem.at[0])
+    load_x = pltpu.make_async_copy(x_hbm, x_buf, load_sem.at[1])
+    load_w.start()
+    load_x.start()
+
+    barrier = pltpu.get_barrier_semaphore()
+    for peer in (partner, ahead, behind):
+        pl.semaphore_signal(barrier, inc=1, device_id=peer, device_id_type=MESH)
+    pl.semaphore_wait(barrier, 3)
+    load_w.wait()
+
     index = lax.broadcasted_iota(jnp.int32, (CHUNK, tok), 0)
-    for b in range(GROUP):
-        m, over, scale = gs_ref[b, 0:1, :], gs_ref[b, 1:2, :], gs_ref[b, 2:3, :]
+
+    def tile(slot, t, dst):
+        gs, cm, lab = gs_ref[t], cm_ref[t], lab_ref[t]
+        m, over, scale = gs[0:1], gs[1:2], gs[2:3]
         for c in range(rows // CHUNK):
             sl = pl.ds(c * CHUNK, CHUNK)
-            p = e_ref[b, sl, :] * (jnp.exp(cm_ref[b, c:c + 1, :] - m) * over)
-            hit = index == lab_ref[b] - c * CHUNK
-            g_ref[b, sl, :] = jnp.where(hit, p - scale, p).astype(BF16)
-    dx = mm(wt_ref[...], side_by_side(g_ref), 1, 0)
-    for b in range(GROUP):
-        dx_ref[b] = dx[:, b * tok:(b + 1) * tok]
-
-
-def grad(wt, e, cm, gs, lab):
+            p = e_buf[slot, sl, :] * (jnp.exp(cm[c:c + 1] - m) * over)
+            g_buf[t, sl, :] = jnp.where(index == lab - c * CHUNK, p - scale, p).astype(BF16)
+        dst[...] = mm(w_buf[...], g_buf[t], 1, 0)
+
+    def pair_copy(i):
+        return pltpu.make_async_remote_copy(
+            src_ref=send_buf.at[lax.rem(i, 2)], dst_ref=pair.at[i], send_sem=pair_send.at[lax.rem(i, 2)],
+            recv_sem=pair_recv.at[i], device_id=partner, device_id_type=MESH)
+
+    def pair_add(i):
+        pair_copy(i).wait_recv()
+        own[i] += pair[i]
+
+    def unit(way, k, h, src):
+        sl = pl.ds(h * half, half)
+        s = way * 8 + k * 2 + h
+        return pltpu.make_async_remote_copy(
+            src_ref=src.at[sl, :], dst_ref=chain.at[way * far + k, sl, :], send_sem=chain_send.at[s], recv_sem=chain_recv.at[s],
+            device_id=ahead if way == 0 else behind, device_id_type=MESH)
+
+    def place(way, k):
+        return 0 if k == 0 else 2 * k - 1 + way
+
+    def first_send(way):
+        unit(way, 0, way, own.at[0]).start()
+
+    def plain_send(way):
+        unit(way, 1, 1 - way, own.at[place(way, 1)]).start()
+
+    def forward(way, k, h):
+        here = chain.at[way * far + k]
+        unit(way, k, h, here).wait_recv()
+        sl = pl.ds(h * half, half)
+        here[sl, :] += own[place(way, k + 1), sl, :]
+        unit(way, k + 1, h, here).start()
+
+    def body(i, carry):
+        load_e(i, 0).wait()
+
+        @pl.when(i >= 2)
+        def _():
+            pair_copy(i - 2).wait_send()
+
+        tile(0, block_at(i, False), send_buf.at[lax.rem(i, 2)])
+        pair_copy(i).start()
+
+        @pl.when(i < chips - 1)
+        def _():
+            load_e(i + 1, 0).start()
+
+        load_e(i, 1).wait()
+        tile(1, block_at(i, True), own.at[i])
+
+        @pl.when(i < chips - 1)
+        def _():
+            load_e(i + 1, 1).start()
+
+        @pl.when(i >= 1)
+        def _():
+            pair_add(i - 1)
+
+        @pl.when(i == 1)
+        def _():
+            first_send(0)
+            first_send(1)
+
+        @pl.when(i == 2)
+        def _():
+            plain_send(0)
+
+        @pl.when(i == 3)
+        def _():
+            plain_send(1)
+
+        @pl.when(i == chips - 2)
+        def _():
+            for way in range(2):
+                forward(way, 0, way)
+        return carry
+
+    lax.fori_loop(0, chips, body, 0)
+    pair_add(chips - 1)
+    for way in range(2):
+        forward(way, 1, 1 - way)
+    load_x.wait()
+    width = dw_ref.shape[1] // 6
+
+    def head(j, carry):
+        for q in range(2):
+            start = pl.multiple_of((2 * j + q) * width, width)
+            g = jnp.concatenate([g_buf[b, pl.ds(start, width), :] for b in range(n)], axis=1)
+            dw_ref[:, pl.ds(start, width)] = mm(side_by_side(x_buf), g, 1, 1).astype(BF16)
+        for k in range(3):
+            @pl.when(j == k)
+            def _():
+                for way in range(2):
+                    if k == 0:
+                        forward(way, 1, way)
+                    if k == 1:
+                        forward(way, 2, 1 - way)
+                    if k == 2:
+                        forward(way, 2, way)
+        return carry
+
+    lax.fori_loop(0, 3, head, 0)
+    for h in range(2):
+        for way in range(2):
+            unit(way, far - 1, h, own.at[0]).wait_recv()
+    dx_ref[...] = own[chips - 1] + (chain[far - 1] + chain[2 * far - 1])
+    for i in range(chips - 2, chips):
+        pair_copy(i).wait_send()
+    for way in range(2):
+        for k in range(far):
+            for h in range(2):
+                if k > 0 or h == way:
+                    unit(way, k, h, own.at[0]).wait_send()
+
+
+def grad(wt, e, x, cm, gs, lab):
     dim, rows = wt.shape
     n, _, tok = e.shape
-    block = lambda r, c: pl.BlockSpec((GROUP, r, c), lambda i: (i, 0, 0))
+    chips = n // 2
+    vmem = pl.BlockSpec(memory_space=pltpu.VMEM)
+    anywhere = pl.BlockSpec(memory_space=pl.ANY)
     return pl.pallas_call(
-        grad_kernel,
-        grid=(n // GROUP,),
-        in_specs=[pl.BlockSpec((dim, rows), lambda i: (0, 0)), block(rows, tok), block(8, tok), block(8, tok), block(1, tok)],
-        out_specs=[block(rows, tok), block(dim, tok)],
-        out_shape=[jax.ShapeDtypeStruct((n, rows, tok), BF16), jax.ShapeDtypeStruct((n, dim, tok), F32)],
-        compiler_params=params(56),
-        cost_estimate=cost(2 * n * tok * dim * rows, 6 * n * tok * rows),
+        functools.partial(grad_kernel, n),
+        in_specs=[anywhere, anywhere, anywhere, vmem, vmem, vmem],
+        out_specs=[vmem, vmem],
+        out_shape=[jax.ShapeDtypeStruct((dim, tok), F32), jax.ShapeDtypeStruct((dim, rows), BF16)],
+        scratch_shapes=[
+            pltpu.VMEM((dim, rows), BF16),
+            pltpu.VMEM((n, dim, tok), BF16),
+            pltpu.VMEM((2, rows, tok), F32),
+            pltpu.VMEM((n, rows, tok), BF16),
+            pltpu.VMEM((2, dim, tok), F32),
+            pltpu.VMEM((chips, dim, tok), F32),
+            pltpu.VMEM((chips, dim, tok), F32),
+            pltpu.VMEM((chips, dim, tok), F32),
+            pltpu.SemaphoreType.DMA((2,)),
+            pltpu.SemaphoreType.DMA((2,)),
+            pltpu.SemaphoreType.DMA((2,)),
+            pltpu.SemaphoreType.DMA((chips,)),
+            pltpu.SemaphoreType.DMA((16,)),
+            pltpu.SemaphoreType.DMA((16,)),
+        ],
+        compiler_params=pltpu.CompilerParams(vmem_limit_bytes=60 * MIB, collective_id=1, has_side_effects=True),
+        cost_estimate=cost(4 * n * tok * dim * rows, 6 * n * tok * rows),
         name='grad',
-    )(wt, e, cm, gs, lab)
-
-
-def head_kernel(x_ref, g_ref, out_ref):
-    out_ref[...] = mm(side_by_side(x_ref), side_by_side(g_ref), 1, 1).astype(BF16)
-
-
-def head(x, g):
-    n, dim, tok = x.shape
-    rows = g.shape[1]
-    tile = 512
-    return pl.pallas_call(
-        head_kernel,
-        grid=(rows // tile,),
-        in_specs=[pl.BlockSpec((n, dim, tok), lambda i: (0, 0, 0)), pl.BlockSpec((n, tile, tok), lambda i: (0, i, 0))],
-        out_specs=pl.BlockSpec((dim, tile), lambda i: (0, i)),
-        out_shape=jax.ShapeDtypeStruct((dim, rows), BF16),
-        compiler_params=params(56),
-        cost_estimate=cost(2 * n * tok * dim * rows, 2 * n * tok * rows),
-        name='head',
-    )(x, g)
+    )(e, wt, x, cm, gs, lab)
 
 
 def solution(mesh):
@@ -296,11 +439,10 @@
         embed_part = embed(ids, e_loc.T)
         embed_rows = lax.psum_scatter(embed_part, 'stage', scatter_dimension=0)
         stage_out = mlp(acts_loc[0].T, up_loc[0], jnp.swapaxes(down_loc[0], 1, 2))
+        lab, stage_out = lax.optimization_barrier((lab, stage_out))
         e, cm, st = logits(wt, x, lab)
         gs, loss = stats(st, mask)
-        g, dx_part = grad(wt, e, cm, gs, lab)
-        dx = lax.psum_scatter(dx_part, 'stage', scatter_dimension=0)
-        dw = head(x, g)
+        dx, dw = grad(wt, e, x, cm, gs, lab)
         return loss[0, :1], dx.T, dw.T, embed_rows.T, stage_out.T[None]
 
     return jax.shard_map(

time: 214 us -> 213 us (level)
  waiting for transfers between devices: 27.1 us -> 0.81 us
  Pallas kernels: 163 us -> 184 us
  local copies, waits for them, and re-layouts: 6.6 us -> 12 us
    all_gather x1, waiting for transfers between devices: 24.7 us -> 0.02 us  [per_device(): x = lax.all_gather(x_loc.T, 'stage', axis=0)]
    pallas_call x2 -> x1, Pallas kernels: 53 us -> 67.6 us  [grad(): pl.pallas_call(functools.partial(grad_kernel, n), in_specs=[anywhere, any...]
    pallas_call x1, Pallas kernels: 17 us -> 23.1 us  [stats(): pl.pallas_call(functools.partial(stats_kernel, n), in_specs=[vmem, vmem],...]
    unnamed x12, local copies, waits for them, and re-layouts: 6.09 us -> 11.4 us
  transfers between devices with their start and end apart: 3 -> 2, of which waited for: 2 -> 0; matrix products, arithmetic and copies ran while one was open for 1% -> 1% of each run, Pallas kernels for 77% -> 87%
where the time goes in v2:
time: 213 us; the launch traced here: 212 us
  Pallas kernels  184 us (86%)
  between operations  14.1 us (7%)
  local copies, waits for them, and re-layouts  12 us (6%)
    pallas_call x1, Pallas kernels, grad(): pl.pallas_call(functools.partial(grad_kernel, n), in_specs=[anywhere, any...  67.6 us
    pallas_call x1, Pallas kernels, mlp(): pl.pallas_call(mlp_kernel, grid=(tokens // tile,), in_specs=[pl.BlockSpec...  41 us
    pallas_call x1, Pallas kernels, logits(): pl.pallas_call(logits_kernel, grid=(n // GROUP,), in_specs=[pl.BlockSpec(...  35.2 us
    pallas_call x1, Pallas kernels, stats(): pl.pallas_call(functools.partial(stats_kernel, n), in_specs=[vmem, vmem],...  23.1 us
    pallas_call x1, Pallas kernels, embed(): pl.pallas_call(embed_kernel, grid=(n // GROUP,), in_specs=[pl.BlockSpec((...  16.9 us
    unnamed x12, local copies, waits for them, and re-layouts  11.4 us
  transfers between devices with their start and end apart: 2, of which 0 were waited for; matrix products, arithmetic and copies ran while one was open for 1% of the time, Pallas kernels for 87%

profile of v2, /device:TPU:21, one launch (start us, length us, event | category | flops | bytes accessed | tf_op | source)
XLA Modules:
  0.0 212.2 jit_solution(17399593242173438222)
XLA Ops:
  7.2 0.1 all-gather.3.cloned.1.call-start
  7.2 0.7 all-gather.3.cloned.1.call-update
  8.0 0.1 reduce-scatter.2.cloned.1.call-start
  8.0 1.3 broadcast_subtract_fusion
  9.4 0.0 copy-start
  9.4 2.0 copy-done
  11.4 16.9 %embed.1 = bf16[16,576,256]{2,1,0:T(8,128)(2,1)} custom-call(s32[16,1,256]{2,1,0:T(1,128)S(1)} %bitcast.24, bf16[576,3072]{1,0:T(8,128)(2,1)S(1)} %bitcast.25), custom_call_target="tpu_custom_call" | custom-call | flops 14495514624 | bytes 8257536 | tf_op jit(solution)/shard_map/embed/pallas_call | solution.py:104
  28.3 0.0 copy-start.1
  28.3 0.1 reduce-scatter.2.cloned.1.call-update
  28.4 1.9 copy-done.1
  30.3 0.0 copy-start.4
  30.3 41.0 %mlp.1 = bf16[576,4096]{1,0:T(8,128)(2,1)} custom-call(bf16[576,4096]{1,0:T(8,128)(2,1)} %bitcast.32, bf16[2,576,1536]{2,1,0:T(8,128)(2,1)S(1)} %bitcast.26, bf16[2,576,1536]{2,1,0:T(8,128)(2,1)} %bitcast.35), custom_call_target="tpu_custom_call" | custom-call | flops 28991029248 | bytes 16515072 | tf_op jit(solution)/shard_map/mlp/pallas_call | solution.py:74
  71.3 0.0 copy-done.4
  71.3 0.0 all-gather.3.cloned.1.call-done
  71.4 35.2 %logits.1 = (f32[16,3072,256]{2,1,0:T(8,128)}, f32[16,8,256]{2,1,0:T(8,128)}, f32[16,8,256]{2,1,0:T(8,128)}) custom-call(bf16[576,3072]{1,0:T(8,128)(2,1)} %bitcast.36, bf16[16,576,256]{2,1,0:T(8,128)(2,1)} %bitcast.33, s32[16,1,256]{2,1,0:T(1,128)} %bitcast.30), custom_call_target="tpu_custom_call" | custom-call | flops 14495514624 | bytes 50331648 | tf_op jit(solution)/shard_map/logits/pallas_call | solution.py:155
  106.5 0.0 copy-start.3
  106.5 0.9 copy-done.3
  107.5 23.1 %stats.1 = (f32[16,8,256]{2,1,0:T(8,128)S(1)}, f32[8,128]{1,0:T(8,128)S(1)}) custom-call(f32[16,8,256]{2,1,0:T(8,128)S(1)} %copy-done.3, f32[16,1,256]{2,1,0:T(1,128)S(1)} %bitcast.23), custom_call_target="tpu_custom_call" | custom-call | flops 1000000000 | bytes 2000000 | tf_op jit(solution)/shard_map/stats/pallas_call | solution.py:214
  130.5 0.0 copy-start.2
  130.5 0.6 copy-done.2
  131.2 0.5 slice.3
  131.7 67.6 %grad.1 = (f32[576,256]{1,0:T(8,128)}, bf16[576,3072]{1,0:T(8,128)(2,1)}) custom-call(f32[16,3072,256]{2,1,0:T(8,128)} %get-tuple-element.17.e_hbm, bf16[576,3072]{1,0:T(8,128)(2,1)} %bitcast.37, bf16[16,576,256]{2,1,0:T(8,128)(2,1)} %bitcast.34, f32[16,8,256]{2,1,0:T(8,128)} %get-tuple-element.18.cm_ref, f32[16,8,256]{2,1,0:T(8,128)} %copy-done.2, ...), custom_call_target="tpu_custom_call" | custom-call | flops 28991029248 | bytes 75497472 | tf_op jit(solution)/shard_map/grad/pallas_call | solution.py:397
  199.3 0.0 reduce-scatter.2.cloned.1.call-done
  199.4 1.9 copy.16
  201.3 4.0 %copy.17 = bf16[3072,576]{0,1:T(8,128)(2,1)} copy(bf16[3072,576]{0,1:T(8,128)(2,1)} %bitcast.27) | data formatting | bytes 7077888
  (1 shorter events, 0.0 us)
Async XLA Ops:
  7.2 64.2 %all-gather.3.cloned.1.call-start = ((), (), s32[]{:S(2)}) async-start(), calls=%async_computation.2 | async-start | bytes 5013504 | tf_op jit(solution)/shard_map/all_gather | solution.py:435
  8.0 191.4 %reduce-scatter.2.cloned.1.call-start = ((), (), s32[]{:S(2)}) async-start(), calls=%async_computation.1 | async-start | bytes 5013504 | tf_op jit(solution)/shard_map/reduce_scatter | solution.py:440
  9.4 2.0 copy-start
  28.3 2.0 copy-start.1
  30.3 41.0 %copy-start.4 = (s32[4096]{0:T(1024)S(1)}, s32[4096]{0:T(1024)}, u32[]{:S(2)}) copy-start(s32[4096]{0:T(1024)} %param.12) | copy-start | bytes 49156
  106.5 0.9 copy-start.3
  130.5 0.7 copy-start.2
Sparse Core Ops, SparseCore 0:
  9.6 44.0 all-gather.2
  56.7 56.4 reduce-scatter.1

commit v3 on v2

--- a/solution.py
+++ b/solution.py
@@ -43,45 +43,50 @@
     return half + half * jnp.tanh(inner)
 
 
+MLP_TILE = 512
+MLP_FIRST = 4
+
+
+def mlp_layers(h, upt_ref, down_ref):
+    for i in range(upt_ref.shape[0]):
+        u = jnp.concatenate(
+            [gelu(mm(upt_ref[i, pl.ds(c, 512), :], h, 1, 0)).astype(BF16) for c in range(0, upt_ref.shape[1], 512)], axis=0)
+        h = (h.astype(F32) + mm(down_ref[i], u, 1, 0)).astype(BF16)
+    return h
+
+
+def is_middle():
+    stage = lax.axis_index('stage')
+    return (stage > 0) & (stage < lax.axis_size('stage') - 1)
+
+
 def mlp_kernel(a_ref, up_ref, down_ref, y_ref, upt_ref):
-    layers = up_ref.shape[0]
-    stage = lax.axis_index('stage')
-    middle = (stage > 0) & (stage < lax.axis_size('stage') - 1)
-
     @pl.when(pl.program_id(0) == 0)
     def _():
-        for i in range(layers):
+        for i in range(up_ref.shape[0]):
             transpose_into(upt_ref.at[i], up_ref[i], 256)
 
-    @pl.when(middle)
+    @pl.when(is_middle())
     def _():
-        h = a_ref[...]
-        for i in range(layers):
-            u = jnp.concatenate(
-                [gelu(mm(upt_ref[i, pl.ds(c, 512), :], h, 1, 0)).astype(BF16) for c in range(0, up_ref.shape[2], 512)], axis=0)
-            h = (h.astype(F32) + mm(down_ref[i], u, 1, 0)).astype(BF16)
-        y_ref[...] = h
-
-    @pl.when(jnp.logical_not(middle))
+        y_ref[...] = mlp_layers(a_ref[...], upt_ref, down_ref)
+
+    @pl.when(jnp.logical_not(is_middle()))
     def _():
         y_ref[...] = a_ref[...]
 
 
 def mlp(at, up, down):
-    dim, tokens = at.shape
+    dim = at.shape[0]
     layers, _, hidden = up.shape
-    tile = 512
+    tokens = MLP_FIRST * MLP_TILE
+    whole = lambda shape: pl.BlockSpec(shape, lambda i: (0, 0, 0))
+    tile = pl.BlockSpec((dim, MLP_TILE), lambda i: (0, i))
     return pl.pallas_call(
         mlp_kernel,
-        grid=(tokens // tile,),
-        in_specs=[
-            pl.BlockSpec((dim, tile), lambda i: (0, i)),
-            pl.BlockSpec((layers, dim, hidden), lambda i: (0, 0, 0)),
-            pl.BlockSpec((layers, dim, hidden), lambda i: (0, 0, 0)),
-        ],
-        out_specs=pl.BlockSpec((dim, tile), lambda i: (0, i)),
-        out_shape=jax.ShapeDtypeStruct((dim, tokens), BF16),
-        scratch_shapes=[pltpu.VMEM((layers, hidden, dim), BF16)],
+        grid=(MLP_FIRST,),
+        in_specs=[tile, whole((layers, dim, hidden)), whole((layers, dim, hidden))],
+        out_specs=[tile, whole((layers, hidden, dim))],
+        out_shape=[jax.ShapeDtypeStruct((dim, tokens), BF16), jax.ShapeDtypeStruct((layers, hidden, dim), BF16)],
         compiler_params=params(48),
         cost_estimate=cost(4 * layers * tokens * dim * hidden, 4 * tokens * dim + 4 * layers * dim * hidden),
         name='mlp',
@@ -226,14 +231,14 @@
     )(st, mask)
 
 
-def grad_kernel(n, e_hbm, w_hbm, x_hbm, cm_ref, gs_ref, lab_ref, dx_ref, dw_ref, w_buf, x_buf, e_buf, g_buf, send_buf, own, pair,
-                chain, load_sem, e_sem, pair_send, pair_recv, chain_send, chain_recv):
+def grad_kernel(n, e_hbm, w_hbm, x_hbm, a_hbm, upt_hbm, down_hbm, cm_ref, gs_ref, lab_ref, dx_ref, dw_hbm, y_hbm, g_buf, send_buf,
+                own, pair, chain, load_sem, e_sem, pair_send, pair_recv, chain_send, chain_recv, a_sem, y_sem):
     stage = lax.axis_index('stage')
     chips = n // 2
     far = chips // 2
     z, core = stage // 2, lax.rem(stage, 2)
     dim, tok = dx_ref.shape
-    rows = w_buf.shape[1]
+    rows = w_hbm.shape[1]
     half = dim // 2
     partner = {'stage': 2 * z + 1 - core}
     ahead = {'stage': 2 * lax.rem(z + 1, chips) + core}
@@ -247,32 +252,10 @@
     def block_at(i, own_side):
         return 2 * chip_at(i) + (core if own_side else 1 - core)
 
-    def load_e(i, slot):
-        return pltpu.make_async_copy(e_hbm.at[block_at(i, slot == 1)], e_buf.at[slot], e_sem.at[slot])
-
-    for slot in range(2):
-        load_e(0, slot).start()
-    load_w = pltpu.make_async_copy(w_hbm, w_buf, load_sem.at[0])
-    load_x = pltpu.make_async_copy(x_hbm, x_buf, load_sem.at[1])
-    load_w.start()
-    load_x.start()
-
     barrier = pltpu.get_barrier_semaphore()
     for peer in (partner, ahead, behind):
         pl.semaphore_signal(barrier, inc=1, device_id=peer, device_id_type=MESH)
     pl.semaphore_wait(barrier, 3)
-    load_w.wait()
-
-    index = lax.broadcasted_iota(jnp.int32, (CHUNK, tok), 0)
-
-    def tile(slot, t, dst):
-        gs, cm, lab = gs_ref[t], cm_ref[t], lab_ref[t]
-        m, over, scale = gs[0:1], gs[1:2], gs[2:3]
-        for c in range(rows // CHUNK):
-            sl = pl.ds(c * CHUNK, CHUNK)
-            p = e_buf[slot, sl, :] * (jnp.exp(cm[c:c + 1] - m) * over)
-            g_buf[t, sl, :] = jnp.where(index == lab - c * CHUNK, p - scale, p).astype(BF16)
-        dst[...] = mm(w_buf[...], g_buf[t], 1, 0)
 
     def pair_copy(i):
         return pltpu.make_async_remote_copy(
@@ -306,75 +289,175 @@
         here[sl, :] += own[place(way, k + 1), sl, :]
         unit(way, k + 1, h, here).start()
 
-    def body(i, carry):
-        load_e(i, 0).wait()
-
-        @pl.when(i >= 2)
-        def _():
-            pair_copy(i - 2).wait_send()
-
-        tile(0, block_at(i, False), send_buf.at[lax.rem(i, 2)])
-        pair_copy(i).start()
-
-        @pl.when(i < chips - 1)
-        def _():
-            load_e(i + 1, 0).start()
-
-        load_e(i, 1).wait()
-        tile(1, block_at(i, True), own.at[i])
-
-        @pl.when(i < chips - 1)
-        def _():
-            load_e(i + 1, 1).start()
-
-        @pl.when(i >= 1)
-        def _():
-            pair_add(i - 1)
-
-        @pl.when(i == 1)
-        def _():
-            first_send(0)
-            first_send(1)
-
-        @pl.when(i == 2)
-        def _():
-            plain_send(0)
-
-        @pl.when(i == 3)
-        def _():
-            plain_send(1)
-
-        @pl.when(i == chips - 2)
-        def _():
-            for way in range(2):
-                forward(way, 0, way)
-        return carry
-
-    lax.fori_loop(0, chips, body, 0)
+    def gradients(w_buf, e_buf):
+        def load_e(i, q):
+            slot = lax.rem(i, 2)
+            return pltpu.make_async_copy(e_hbm.at[block_at(i, q == 1)], e_buf.at[slot, q], e_sem.at[slot, q])
+
+        for q in range(2):
+            load_e(0, q).start()
+        load_w = pltpu.make_async_copy(w_hbm, w_buf, load_sem.at[0])
+        load_w.start()
+        index = lax.broadcasted_iota(jnp.int32, (CHUNK, tok), 0)
+        load_w.wait()
+
+        def body(i, carry):
+            @pl.when(i < chips - 1)
+            def _():
+                for q in range(2):
+                    load_e(i + 1, q).start()
+
+            @pl.when(i >= 2)
+            def _():
+                pair_copy(i - 2).wait_send()
+
+            for q in range(2):
+                load_e(i, q).wait()
+            slot = lax.rem(i, 2)
+            blocks = [block_at(i, q == 1) for q in range(2)]
+            parts = [[], []]
+            for q in range(2):
+                gs, cm, lab = gs_ref[blocks[q]], cm_ref[blocks[q]], lab_ref[blocks[q]]
+                m, over, scale = gs[0:1], gs[1:2], gs[2:3]
+                for c in range(rows // CHUNK):
+                    sl = pl.ds(c * CHUNK, CHUNK)
+                    p = e_buf[slot, q, sl, :] * (jnp.exp(cm[c:c + 1] - m) * over)
+                    g = jnp.where(index == lab - c * CHUNK, p - scale, p).astype(BF16)
+                    g_buf[blocks[q], sl, :] = g
+                    parts[q].append(g)
+            both = jnp.concatenate([jnp.concatenate(p, axis=0) for p in parts], axis=1)
+            dx = mm(w_buf[...], both, 1, 0)
+            send_buf[slot] = dx[:, :tok]
+            own[i] = dx[:, tok:]
+            pair_copy(i).start()
+
+            @pl.when(i >= 1)
+            def _():
+                pair_add(i - 1)
+
+            @pl.when(i == 1)
+            def _():
+                first_send(0)
+                first_send(1)
+
+            @pl.when(i == 2)
+            def _():
+                plain_send(0)
+
+            @pl.when(i == 3)
+            def _():
+                plain_send(1)
+
+            @pl.when(i == chips - 2)
+            def _():
+                for way in range(2):
+                    forward(way, 0, way)
+            return carry
+
+        lax.fori_loop(0, chips, body, 0)
+
+    pl.run_scoped(gradients, pltpu.VMEM((dim, rows), BF16), pltpu.VMEM((2, 2, rows, tok), F32))
     pair_add(chips - 1)
-    for way in range(2):
-        forward(way, 1, 1 - way)
-    load_x.wait()
-    width = dw_ref.shape[1] // 6
-
-    def head(j, carry):
-        for q in range(2):
-            start = pl.multiple_of((2 * j + q) * width, width)
+
+    def fill(x_buf, upt_buf, down_buf, a_buf, y_buf, dw_buf):
+        loads = [
+            pltpu.make_async_copy(src, dst, load_sem.at[k])
+            for k, (src, dst) in enumerate([(x_hbm, x_buf), (upt_hbm, upt_buf), (down_hbm, down_buf)])
+        ]
+        for load in loads:
+            load.start()
+        tiles = y_hbm.shape[1] // MLP_TILE
+
+        def cols(m):
+            return pl.ds(pl.multiple_of(m * MLP_TILE, MLP_TILE), MLP_TILE)
+
+        def load_a(m):
+            slot = lax.rem(m, 2)
+            return pltpu.make_async_copy(a_hbm.at[:, cols(m + MLP_FIRST)], a_buf.at[slot], a_sem.at[slot])
+
+        def store_y(m):
+            slot = lax.rem(m, 2)
+            return pltpu.make_async_copy(y_buf.at[slot], y_hbm.at[:, cols(m)], y_sem.at[slot])
+
+        load_a(0).start()
+        loads[0].wait()
+        width = 512
+        pieces = rows // width
+
+        def store_dw(j):
+            slot = lax.rem(j, 2)
+            start = pl.multiple_of(j * width, width)
+            return pltpu.make_async_copy(dw_buf.at[slot], dw_hbm.at[:, pl.ds(start, width)], y_sem.at[slot])
+
+        def head(j, carry):
+            start = pl.multiple_of(j * width, width)
             g = jnp.concatenate([g_buf[b, pl.ds(start, width), :] for b in range(n)], axis=1)
-            dw_ref[:, pl.ds(start, width)] = mm(side_by_side(x_buf), g, 1, 1).astype(BF16)
-        for k in range(3):
-            @pl.when(j == k)
+
+            @pl.when(j >= 2)
+            def _():
+                store_dw(j - 2).wait()
+
+            dw_buf[lax.rem(j, 2)] = mm(side_by_side(x_buf), g, 1, 1).astype(BF16)
+            store_dw(j).start()
+
+            @pl.when(j == 0)
             def _():
                 for way in range(2):
-                    if k == 0:
-                        forward(way, 1, way)
-                    if k == 1:
-                        forward(way, 2, 1 - way)
-                    if k == 2:
-                        forward(way, 2, way)
-        return carry
-
-    lax.fori_loop(0, 3, head, 0)
+                    forward(way, 1, 1 - way)
+
+            @pl.when(j == 2)
+            def _():
+                for way in range(2):
+                    forward(way, 1, way)
+
+            @pl.when(j == 4)
+            def _():
+                for way in range(2):
+                    forward(way, 2, 1 - way)
+            return carry
+
+        lax.fori_loop(0, pieces, head, 0)
+        for j in range(pieces - 2, pieces):
+            store_dw(j).wait()
+        loads[1].wait()
+        loads[2].wait()
+
+        def layers(m, carry):
+            slot = lax.rem(m, 2)
+
+            @pl.when(m < tiles - 1)
+            def _():
+                load_a(m + 1).start()
+
+            load_a(m).wait()
+
+            @pl.when(m >= 2)
+            def _():
+                store_y(m - 2).wait()
+
+            @pl.when(is_middle())
+            def _():
+                y_buf[slot] = mlp_layers(a_buf[slot], upt_buf, down_buf)
+
+            @pl.when(jnp.logical_not(is_middle()))
+            def _():
+                y_buf[slot] = a_buf[slot]
+
+            store_y(m).start()
+
+            @pl.when(m == 0)
+            def _():
+                for way in range(2):
+                    forward(way, 2, way)
+            return carry
+
+        lax.fori_loop(0, tiles, layers, 0)
+        for m in range(tiles - 2, tiles):
+            store_y(m).wait()
+
+    pl.run_scoped(
+        fill, pltpu.VMEM(x_hbm.shape, BF16), pltpu.VMEM(upt_hbm.shape, BF16), pltpu.VMEM(down_hbm.shape, BF16),
+        pltpu.VMEM((2, dim, MLP_TILE), BF16), pltpu.VMEM((2, dim, MLP_TILE), BF16), pltpu.VMEM((2, dim, 512), BF16))
     for h in range(2):
         for way in range(2):
             unit(way, far - 1, h, own.at[0]).wait_recv()
@@ -388,37 +471,35 @@
                     unit(way, k, h, own.at[0]).wait_send()
 
 
-def grad(wt, e, x, cm, gs, lab):
+def grad(wt, e, x, at, upt, down, cm, gs, lab):
     dim, rows = wt.shape
     n, _, tok = e.shape
     chips = n // 2
+    tokens = at.shape[1] - MLP_FIRST * MLP_TILE
     vmem = pl.BlockSpec(memory_space=pltpu.VMEM)
     anywhere = pl.BlockSpec(memory_space=pl.ANY)
+    dma = pltpu.SemaphoreType.DMA
     return pl.pallas_call(
         functools.partial(grad_kernel, n),
-        in_specs=[anywhere, anywhere, anywhere, vmem, vmem, vmem],
-        out_specs=[vmem, vmem],
-        out_shape=[jax.ShapeDtypeStruct((dim, tok), F32), jax.ShapeDtypeStruct((dim, rows), BF16)],
+        in_specs=[anywhere] * 6 + [vmem] * 3,
+        out_specs=[vmem, anywhere, anywhere],
+        out_shape=[
+            jax.ShapeDtypeStruct((dim, tok), F32),
+            jax.ShapeDtypeStruct((dim, rows), BF16),
+            jax.ShapeDtypeStruct((dim, tokens), BF16),
+        ],
         scratch_shapes=[
-            pltpu.VMEM((dim, rows), BF16),
-            pltpu.VMEM((n, dim, tok), BF16),
-            pltpu.VMEM((2, rows, tok), F32),
             pltpu.VMEM((n, rows, tok), BF16),
             pltpu.VMEM((2, dim, tok), F32),
             pltpu.VMEM((chips, dim, tok), F32),
             pltpu.VMEM((chips, dim, tok), F32),
             pltpu.VMEM((chips, dim, tok), F32),
-            pltpu.SemaphoreType.DMA((2,)),
-            pltpu.SemaphoreType.DMA((2,)),
-            pltpu.SemaphoreType.DMA((2,)),
-            pltpu.SemaphoreType.DMA((chips,)),
-            pltpu.SemaphoreType.DMA((16,)),
-            pltpu.SemaphoreType.DMA((16,)),
+            dma((3,)), dma((2, 2)), dma((2,)), dma((chips,)), dma((16,)), dma((16,)), dma((2,)), dma((2,)),
         ],
-        compiler_params=pltpu.CompilerParams(vmem_limit_bytes=60 * MIB, collective_id=1, has_side_effects=True),
-        cost_estimate=cost(4 * n * tok * dim * rows, 6 * n * tok * rows),
+        compiler_params=pltpu.CompilerParams(vmem_limit_bytes=63 * MIB, collective_id=1, has_side_effects=True),
+        cost_estimate=cost(6 * n * tok * dim * rows, 6 * n * tok * rows),
         name='grad',
-    )(e, wt, x, cm, gs, lab)
+    )(e, wt, x, at, upt, down, cm, gs, lab)
 
 
 def solution(mesh):
@@ -438,11 +519,13 @@
         mask = loss_mask.astype(F32).reshape(n, 1, tok)
         embed_part = embed(ids, e_loc.T)
         embed_rows = lax.psum_scatter(embed_part, 'stage', scatter_dimension=0)
-        stage_out = mlp(acts_loc[0].T, up_loc[0], jnp.swapaxes(down_loc[0], 1, 2))
-        lab, stage_out = lax.optimization_barrier((lab, stage_out))
+        at, down = acts_loc[0].T, jnp.swapaxes(down_loc[0], 1, 2)
+        y0, upt = mlp(at, up_loc[0], down)
+        lab, y0 = lax.optimization_barrier((lab, y0))
         e, cm, st = logits(wt, x, lab)
         gs, loss = stats(st, mask)
-        dx, dw = grad(wt, e, x, cm, gs, lab)
+        dx, dw, y1 = grad(wt, e, x, at, upt, down, cm, gs, lab)
+        stage_out = jnp.concatenate([y0, y1], axis=1)
         return loss[0, :1], dx.T, dw.T, embed_rows.T, stage_out.T[None]
 
     return jax.shard_map(

time: 213 us -> 202 us (0.948)
  Pallas kernels: 184 us -> 169 us
  other arithmetic: 1.34 us -> 6.63 us
    pallas_call x2, Pallas kernels: 109 us -> 93 us  [the longest x1 69.2 us: grad(): pl.pallas_call(functools.partial(grad_kernel, n), in_specs=[anywhere] * 6...]
    broadcast_in_dim x0 -> x1, other arithmetic: none -> 5.28 us  [per_device(): return (loss[0, :1], dx.T, dw.T, embed_rows.T, stage_out.T[None])]
    unnamed x12 -> x16, local copies, waits for them, and re-layouts: 11.4 us -> 10.6 us
  transfers between devices with their start and end apart: 2 -> 2, of which waited for: 0 -> 0; matrix products, arithmetic and copies ran while one was open for 1% -> 4% of each run, Pallas kernels for 87% -> 84%
where the time goes in v3:
time: 202 us
  Pallas kernels  169 us (84%)
  between operations  14.1 us (7%)
  local copies, waits for them, and re-layouts  11.1 us (5%)
  other arithmetic  6.63 us (3%)
    pallas_call x1, Pallas kernels, grad(): pl.pallas_call(functools.partial(grad_kernel, n), in_specs=[anywhere] * 6...  69.2 us
    pallas_call x1, Pallas kernels, logits(): pl.pallas_call(logits_kernel, grid=(n // GROUP,), in_specs=[pl.BlockSpec(...  35.2 us
    pallas_call x1, Pallas kernels, stats(): pl.pallas_call(functools.partial(stats_kernel, n), in_specs=[vmem, vmem],...  24.1 us
    pallas_call x1, Pallas kernels, mlp(): pl.pallas_call(mlp_kernel, grid=(MLP_FIRST,), in_specs=[tile, whole((laye...  23.8 us
    pallas_call x1, Pallas kernels, embed(): pl.pallas_call(embed_kernel, grid=(n // GROUP,), in_specs=[pl.BlockSpec((...  16.9 us
    unnamed x16, local copies, waits for them, and re-layouts  10.6 us
    broadcast_in_dim x1, other arithmetic, per_device(): return (loss[0, :1], dx.T, dw.T, embed_rows.T, stage_out.T[None])  5.28 us
  transfers between devices with their start and end apart: 2, of which 0 were waited for; matrix products, arithmetic and copies ran while one was open for 4% of the time, Pallas kernels for 84%

profile of v3, /device:TPU:21, one launch (start us, length us, event | category | flops | bytes accessed | tf_op | source)
XLA Modules:
  0.0 202.0 jit_solution(10863353228603211636)
XLA Ops:
  7.2 0.1 all-gather.3.cloned.1.call-start
  7.2 0.7 all-gather.3.cloned.1.call-update
  8.0 0.1 reduce-scatter.2.cloned.1.call-start
  8.0 1.3 broadcast_subtract_fusion
  9.4 0.0 copy-start.1
  9.4 2.0 copy-done.1
  11.4 16.9 %embed.1 = bf16[16,576,256]{2,1,0:T(8,128)(2,1)} custom-call(s32[16,1,256]{2,1,0:T(1,128)S(1)} %bitcast.25, bf16[576,3072]{1,0:T(8,128)(2,1)S(1)} %bitcast.26), custom_call_target="tpu_custom_call" | custom-call | flops 14495514624 | bytes 8257536 | tf_op jit(solution)/shard_map/embed/pallas_call | solution.py:109
  28.3 0.0 copy-start.2
  28.3 0.1 reduce-scatter.2.cloned.1.call-update
  28.4 1.9 copy-done.2
  30.3 0.0 copy-start.6
  30.3 23.8 %mlp.1 = (bf16[576,2048]{1,0:T(8,128)(2,1)S(1)}, bf16[2,1536,576]{2,1,0:T(8,128)(2,1)}) custom-call(bf16[576,4096]{1,0:T(8,128)(2,1)} %bitcast.33, bf16[2,576,1536]{2,1,0:T(8,128)(2,1)S(1)} %bitcast.27, bf16[2,576,1536]{2,1,0:T(8,128)(2,1)} %bitcast.39), custom_call_target="tpu_custom_call" | custom-call | flops 14495514624 | bytes 11796480 | tf_op jit(solution)/shard_map/mlp/pallas_call | solution.py:84
  54.1 0.0 copy-start
  54.1 1.4 copy-done
  55.5 0.0 copy-done.6
  55.5 0.0 all-gather.3.cloned.1.call-done
  55.5 35.2 %logits.1 = (f32[16,3072,256]{2,1,0:T(8,128)}, f32[16,8,256]{2,1,0:T(8,128)}, f32[16,8,256]{2,1,0:T(8,128)}) custom-call(bf16[576,3072]{1,0:T(8,128)(2,1)} %bitcast.37, bf16[16,576,256]{2,1,0:T(8,128)(2,1)} %bitcast.35, s32[16,1,256]{2,1,0:T(1,128)} %bitcast.31), custom_call_target="tpu_custom_call" | custom-call | flops 14495514624 | bytes 50331648 | tf_op jit(solution)/shard_map/logits/pallas_call | solution.py:160
  90.7 0.0 copy-start.4
  90.7 0.9 copy-done.4
  91.6 24.1 %stats.1 = (f32[16,8,256]{2,1,0:T(8,128)S(1)}, f32[8,128]{1,0:T(8,128)S(1)}) custom-call(f32[16,8,256]{2,1,0:T(8,128)S(1)} %copy-done.4, f32[16,1,256]{2,1,0:T(1,128)S(1)} %bitcast.24), custom_call_target="tpu_custom_call" | custom-call | flops 1000000000 | bytes 2000000 | tf_op jit(solution)/shard_map/stats/pallas_call | solution.py:219
  115.7 0.0 copy-start.3
  115.7 0.6 copy-done.3
  116.4 0.5 slice.3
  116.9 69.2 %grad.1 = (f32[576,256]{1,0:T(8,128)}, bf16[576,3072]{1,0:T(8,128)(2,1)}, bf16[576,2048]{1,0:T(8,128)(2,1)}) custom-call(f32[16,3072,256]{2,1,0:T(8,128)} %get-tuple-element.21.e_hbm, bf16[576,3072]{1,0:T(8,128)(2,1)} %bitcast.38, bf16[16,576,256]{2,1,0:T(8,128)(2,1)} %bitcast.36, bf16[576,4096]{1,0:T(8,128)(2,1)} %bitcast.34, ...), custom_call_target="tpu_custom_call" | custom-call | flops 43486543872 | bytes 75497472 | tf_op jit(solution)/shard_map/grad/pallas_call | solution.py:482
  186.1 0.0 copy-start.5
  186.1 5.3 %maximum_bitcast_fusion = bf16[1,4096,576]{1,2,0:T(8,128)(2,1)} fusion(bf16[576,2048]{1,0:T(8,128)(2,1)} %get-tuple-element.28, bf16[576,2048]{1,0:T(8,128)(2,1)} %copy-done), kind=kLoop, calls=%fused_computation | loop fusion | flops 9437184 | bytes 9437184 | tf_op jit(solution)/shard_map/broadcast_in_dim | solution.py:529
  191.4 0.0 reduce-scatter.2.cloned.1.call-done
  191.4 1.9 copy.16
  193.3 0.0 copy-done.5
  193.3 1.8 copy.17
  (1 shorter events, 0.0 us)
Async XLA Ops:
  7.2 48.3 %all-gather.3.cloned.1.call-start = ((), (), s32[]{:S(2)}) async-start(), calls=%async_computation.2 | async-start | bytes 5013504 | tf_op jit(solution)/shard_map/all_gather | solution.py:516
  8.0 183.4 %reduce-scatter.2.cloned.1.call-start = ((), (), s32[]{:S(2)}) async-start(), calls=%async_computation.1 | async-start | bytes 5013504 | tf_op jit(solution)/shard_map/reduce_scatter | solution.py:521
  9.4 2.0 copy-start.1
  28.3 2.0 copy-start.2
  30.3 25.2 %copy-start.6 = (s32[4096]{0:T(1024)S(1)}, s32[4096]{0:T(1024)}, u32[]{:S(2)}) copy-start(s32[4096]{0:T(1024)} %param.12) | copy-start | bytes 49156
  54.1 1.4 copy-start
  90.7 0.9 copy-start.4
  115.7 0.7 copy-start.3
  186.1 7.2 %copy-start.5 = (bf16[576,3072]{1,0:T(8,128)(2,1)S(1)}, bf16[576,3072]{1,0:T(8,128)(2,1)}, u32[]{:S(2)}) copy-start(bf16[576,3072]{1,0:T(8,128)(2,1)} %get-tuple-element.26) | copy-start | bytes 10616836
Sparse Core Ops, SparseCore 0:
  9.6 44.0 all-gather.2
  56.7 60.8 reduce-scatter.1

commit v4 on v3

--- a/solution.py
+++ b/solution.py
@@ -44,15 +44,15 @@
 
 
 MLP_TILE = 512
-MLP_FIRST = 4
-
-
-def mlp_layers(h, upt_ref, down_ref):
-    for i in range(upt_ref.shape[0]):
-        u = jnp.concatenate(
-            [gelu(mm(upt_ref[i, pl.ds(c, 512), :], h, 1, 0)).astype(BF16) for c in range(0, upt_ref.shape[1], 512)], axis=0)
-        h = (h.astype(F32) + mm(down_ref[i], u, 1, 0)).astype(BF16)
-    return h
+MLP_GATHER = 1
+MLP_STATS = 5
+
+
+def mlp_layer(h, upt, down):
+    hidden = upt.shape[0]
+    u = jnp.concatenate(
+        [gelu(mm(upt[pl.ds(c, 512), :], h, 1, 0)).astype(BF16) for c in range(0, hidden, 512)], axis=0)
+    return (h.astype(F32) + mm(down[...], u, 1, 0)).astype(BF16)
 
 
 def is_middle():
@@ -60,65 +60,196 @@
     return (stage > 0) & (stage < lax.axis_size('stage') - 1)
 
 
-def mlp_kernel(a_ref, up_ref, down_ref, y_ref, upt_ref):
-    @pl.when(pl.program_id(0) == 0)
-    def _():
-        for i in range(up_ref.shape[0]):
-            transpose_into(upt_ref.at[i], up_ref[i], 256)
-
+def mlp_step(src, dst, upt, down):
     @pl.when(is_middle())
     def _():
-        y_ref[...] = mlp_layers(a_ref[...], upt_ref, down_ref)
+        dst[...] = mlp_layer(src[...], upt, down)
 
     @pl.when(jnp.logical_not(is_middle()))
     def _():
-        y_ref[...] = a_ref[...]
-
-
-def mlp(at, up, down):
-    dim = at.shape[0]
+        dst[...] = src[...]
+
+
+class Place:
+    def __init__(self, n):
+        stage = lax.axis_index('stage')
+        self.chips = n // 2
+        self.far = self.chips // 2
+        self.z, self.core = stage // 2, lax.rem(stage, 2)
+        self.partner = {'stage': 2 * self.z + 1 - self.core}
+        self.along = [{'stage': 2 * self.chip(1) + self.core}, {'stage': 2 * self.chip(-1) + self.core}]
+
+    def chip(self, steps):
+        return lax.rem(self.z + steps + self.chips, self.chips)
+
+    def block(self, chip, own_side):
+        return 2 * chip + (self.core if own_side else 1 - self.core)
+
+    def greet(self, barrier):
+        for peer in [self.partner] + self.along:
+            pl.semaphore_signal(barrier, inc=1, device_id=peer, device_id_type=MESH)
+        pl.semaphore_wait(barrier, 3)
+
+
+def gather_kernel(n, x_ref, ids_ref, et_hbm, up_hbm, down_hbm, a_hbm, x_out, h_out, y_out, upt_out, x_all, et, up_buf, upt_buf,
+                  down_buf, a_buf, y_buf, send_buf, own, pair, load_sem, out_sem, ring_send, ring_recv, side_send, side_recv,
+                  pair_send, pair_recv):
+    here = Place(n)
+    dim, tok = x_ref.shape
+    half = dim // 2
+    rows = et.shape[1]
+    layers = up_buf.shape[0]
+    mine = here.block(here.z, True)
+    loads = [
+        pltpu.make_async_copy(src, dst, load_sem.at[k])
+        for k, (src, dst) in enumerate([
+            (et_hbm, et), (up_hbm, up_buf), (down_hbm, down_buf), (a_hbm.at[:, pl.ds(0, MLP_TILE)], a_buf), (x_ref, x_all.at[mine])])
+    ]
+    for load in loads:
+        load.start()
+    here.greet(pltpu.get_barrier_semaphore())
+
+    def unit(way, k, h):
+        sl = pl.ds(h * half, half)
+        block = here.block(here.chip(k if way else -k), True)
+        src = x_ref.at[sl, :] if k == 0 else x_all.at[block, sl, :]
+        s = way * 8 + k * 2 + h
+        return pltpu.make_async_remote_copy(
+            src_ref=src, dst_ref=x_all.at[block, sl, :], send_sem=ring_send.at[s], recv_sem=ring_recv.at[s],
+            device_id=here.along[way], device_id_type=MESH)
+
+    def side(way, k, h):
+        sl = pl.ds(h * half, half)
+        block = here.block(here.chip(1 + k if way else -1 - k), True)
+        s = way * 8 + k * 2 + h
+        return pltpu.make_async_remote_copy(
+            src_ref=x_all.at[block, sl, :], dst_ref=x_all.at[block, sl, :], send_sem=side_send.at[s], recv_sem=side_recv.at[s],
+            device_id=here.partner, device_id_type=MESH)
+
+    def side_mine():
+        return pltpu.make_async_remote_copy(
+            src_ref=x_ref, dst_ref=x_all.at[mine], send_sem=side_send.at[16], recv_sem=side_recv.at[16],
+            device_id=here.partner, device_id_type=MESH)
+
+    last = here.far - 1
+    arrivals = [[(k, h) for k in range(last) for h in range(2)] + [(last, way)] for way in range(2)]
+
+    def event(u):
+        for way in range(2):
+            k, h = arrivals[way][u]
+            unit(way, k, h).wait_recv()
+            if (k + 1, h) in arrivals[way]:
+                unit(way, k + 1, h).start()
+            side(way, k, h).start()
+
+    for h in range(2):
+        for way in range(2):
+            unit(way, 0, h).start()
+    side_mine().start()
+
+    def pair_copy(i):
+        return pltpu.make_async_remote_copy(
+            src_ref=send_buf.at[lax.rem(i, 2)], dst_ref=pair.at[i], send_sem=pair_send.at[lax.rem(i, 2)],
+            recv_sem=pair_recv.at[i], device_id=here.partner, device_id_type=MESH)
+
+    def pair_add(i):
+        pair_copy(i).wait_recv()
+        own[i] = (own[i].astype(F32) + pair[i].astype(F32)).astype(BF16)
+
+    loads[0].wait()
+    index = lax.broadcasted_iota(jnp.int32, (rows, 2 * tok), 0)
+
+    def embed(i, carry):
+        @pl.when(i >= 2)
+        def _():
+            pair_copy(i - 2).wait_send()
+
+        ids = jnp.concatenate([ids_ref[here.block(i, False)], ids_ref[here.block(i, True)]], axis=1)
+        hot = jnp.where(index == ids, 1.0, 0.0).astype(BF16)
+        out = mm(et[...], hot, 1, 0).astype(BF16)
+        send_buf[lax.rem(i, 2)] = out[:, :tok]
+        own[i] = out[:, tok:]
+        pair_copy(i).start()
+
+        @pl.when(i >= 1)
+        def _():
+            pair_add(i - 1)
+
+        for u in range(here.chips - 2):
+            @pl.when(i == u + 2)
+            def _():
+                event(u)
+        return carry
+
+    lax.fori_loop(0, here.chips, embed, 0)
+    loads[1].wait()
+    for i in range(layers):
+        transpose_into(upt_buf.at[i], up_buf[i], 256)
+    loads[2].wait()
+    loads[3].wait()
+    mlp_step(a_buf, y_buf, upt_buf.at[0], down_buf.at[0])
+    event(here.chips - 2)
+    pair_add(here.chips - 1)
+    outs = [
+        pltpu.make_async_copy(src, dst, out_sem.at[k])
+        for k, (src, dst) in enumerate([(own, h_out), (upt_buf, upt_out), (x_all, x_out), (y_buf, y_out)])
+    ]
+    outs[0].start()
+    outs[1].start()
+    loads[4].wait()
+    side_mine().wait()
+    for way in range(2):
+        for k, h in arrivals[way]:
+            side(way, k, h).wait()
+    outs[2].start()
+    for i in range(1, layers):
+        mlp_step(y_buf, y_buf, upt_buf.at[i], down_buf.at[i])
+    outs[3].start()
+    for way in range(2):
+        for k, h in arrivals[way]:
+            unit(way, k, h).wait_send()
+    for i in range(here.chips - 2, here.chips):
+        pair_copy(i).wait_send()
+    for out in outs:
+        out.wait()
+
+
+def gather(xt, ids, et, up, down, at):
+    dim, tok = xt.shape
+    n = ids.shape[0]
+    rows = et.shape[1]
     layers, _, hidden = up.shape
-    tokens = MLP_FIRST * MLP_TILE
-    whole = lambda shape: pl.BlockSpec(shape, lambda i: (0, 0, 0))
-    tile = pl.BlockSpec((dim, MLP_TILE), lambda i: (0, i))
+    tokens = MLP_GATHER * MLP_TILE
+    vmem = pl.BlockSpec(memory_space=pltpu.VMEM)
+    anywhere = pl.BlockSpec(memory_space=pl.ANY)
+    dma = pltpu.SemaphoreType.DMA
     return pl.pallas_call(
-        mlp_kernel,
-        grid=(MLP_FIRST,),
-        in_specs=[tile, whole((layers, dim, hidden)), whole((layers, dim, hidden))],
-        out_specs=[tile, whole((layers, hidden, dim))],
-        out_shape=[jax.ShapeDtypeStruct((dim, tokens), BF16), jax.ShapeDtypeStruct((layers, hidden, dim), BF16)],
-        compiler_params=params(48),
-        cost_estimate=cost(4 * layers * tokens * dim * hidden, 4 * tokens * dim + 4 * layers * dim * hidden),
-        name='mlp',
-    )(at, up, down)
-
-
-def embed_kernel(ids_ref, et_ref, out_ref):
-    rows = et_ref.shape[1]
-    tok = ids_ref.shape[2]
-    index = lax.broadcasted_iota(jnp.int32, (rows, GROUP * tok), 0)
-    hot = jnp.where(index == side_by_side(ids_ref), 1.0, 0.0).astype(BF16)
-    out = mm(et_ref[...], hot, 1, 0).astype(BF16)
-    for b in range(GROUP):
-        out_ref[b] = out[:, b * tok:(b + 1) * tok]
-
-
-def embed(ids, et):
-    n, _, tok = ids.shape
-    dim, rows = et.shape
-    return pl.pallas_call(
-        embed_kernel,
-        grid=(n // GROUP,),
-        in_specs=[
-            pl.BlockSpec((GROUP, 1, tok), lambda i: (i, 0, 0)),
-            pl.BlockSpec((dim, rows), lambda i: (0, 0)),
+        functools.partial(gather_kernel, n),
+        in_specs=[vmem, vmem] + [anywhere] * 4,
+        out_specs=[anywhere] * 4,
+        out_shape=[
+            jax.ShapeDtypeStruct((n, dim, tok), BF16),
+            jax.ShapeDtypeStruct((n // 2, dim, tok), BF16),
+            jax.ShapeDtypeStruct((dim, tokens), BF16),
+            jax.ShapeDtypeStruct((layers, hidden, dim), BF16),
         ],
-        out_specs=pl.BlockSpec((GROUP, dim, tok), lambda i: (i, 0, 0)),
-        out_shape=jax.ShapeDtypeStruct((n, dim, tok), BF16),
-        compiler_params=params(48),
-        cost_estimate=cost(2 * n * tok * dim * rows, 2 * dim * (n * tok + rows)),
-        name='embed',
-    )(ids, et)
+        scratch_shapes=[
+            pltpu.VMEM((n, dim, tok), BF16),
+            pltpu.VMEM((dim, rows), BF16),
+            pltpu.VMEM((layers, dim, hidden), BF16),
+            pltpu.VMEM((layers, hidden, dim), BF16),
+            pltpu.VMEM((layers, dim, hidden), BF16),
+            pltpu.VMEM((dim, tokens), BF16),
+            pltpu.VMEM((dim, tokens), BF16),
+            pltpu.VMEM((2, dim, tok), BF16),
+            pltpu.VMEM((n // 2, dim, tok), BF16),
+            pltpu.VMEM((n // 2, dim, tok), BF16),
+            dma((5,)), dma((4,)), dma((16,)), dma((16,)), dma((17,)), dma((17,)), dma((2,)), dma((n // 2,)),
+        ],
+        compiler_params=params(56, collective_id=2, has_side_effects=True),
+        cost_estimate=cost(2 * n * tok * dim * rows, 4 * n * tok * dim),
+        name='gather',
+    )(xt, ids, et, up, down, at)
 
 
 def logits_kernel(wt_ref, x_ref, lab_ref, e_ref, cm_ref, st_ref, w_ref):
@@ -174,8 +305,32 @@
     )(wt, x, lab)
 
 
-def stats_kernel(n, st_ref, mask_ref, out_ref, loss_ref, got, every, send1, recv1, send2, recv2):
+def stats_kernel(n, st_ref, mask_ref, h_hbm, a_hbm, upt_hbm, down_hbm, out_ref, loss_ref, h_ref, y_hbm, got, every, own, chain,
+                 upt_buf, down_buf, a_buf, y_buf, send1, recv1, send2, recv2, load_sem, chain_send, chain_recv, a_sem, y_sem):
+    here = Place(n)
     me = lax.axis_index('stage')
+    dim = h_ref.shape[0]
+    half = dim // 2
+    far = here.far
+    layers = upt_buf.shape[0]
+    loads = [
+        pltpu.make_async_copy(src, dst, load_sem.at[k])
+        for k, (src, dst) in enumerate([(h_hbm, own), (upt_hbm, upt_buf), (down_hbm, down_buf)])
+    ]
+    for load in loads:
+        load.start()
+
+    def load_a(m):
+        start = pl.multiple_of((m + MLP_GATHER) * MLP_TILE, MLP_TILE)
+        slot = lax.rem(m, 2)
+        return pltpu.make_async_copy(a_hbm.at[:, pl.ds(start, MLP_TILE)], a_buf.at[slot], a_sem.at[slot])
+
+    def store_y(m):
+        slot = lax.rem(m, 2)
+        start = pl.multiple_of(m * MLP_TILE, MLP_TILE)
+        return pltpu.make_async_copy(y_buf.at[slot], y_hbm.at[:, pl.ds(start, MLP_TILE)], y_sem.at[slot])
+
+    load_a(0).start()
     barrier = pltpu.get_barrier_semaphore()
     peers = [lax.rem(me + d, n) for d in range(n)]
     for d in range(1, n):
@@ -188,47 +343,147 @@
             src_ref=st_ref.at[peers[d]], dst_ref=got.at[d], send_sem=send1.at[d], recv_sem=recv1.at[d],
             device_id={'stage': peers[d]}, device_id_type=MESH))
         first[-1].start()
+
+    def target_chip(way, k):
+        return here.chip(far - k if way == 0 else k - far)
+
+    def unit(way, k, h, src):
+        sl = pl.ds(h * half, half)
+        s = way * 8 + k * 2 + h
+        return pltpu.make_async_remote_copy(
+            src_ref=src.at[sl, :], dst_ref=chain.at[way * far + k, sl, :], send_sem=chain_send.at[s], recv_sem=chain_recv.at[s],
+            device_id=here.along[way], device_id_type=MESH)
+
+    def forward(way, k, h):
+        arrived = chain.at[way * far + k]
+        unit(way, k, h, arrived).wait_recv()
+        sl = pl.ds(h * half, half)
+        arrived[sl, :] = (arrived[sl, :].astype(F32) + own[target_chip(way, k + 1), sl, :].astype(F32)).astype(BF16)
+        unit(way, k + 1, h, arrived).start()
+
+    loads[0].wait()
+    for way in range(2):
+        unit(way, 0, way, own.at[target_chip(way, 0)]).start()
+    for way in range(2):
+        unit(way, 1, 1 - way, own.at[target_chip(way, 1)]).start()
+
     weight = mask_ref[...]
     count = jnp.maximum(jnp.sum(weight, keepdims=True)[0], 1.0)
-    for copy in first:
-        copy.wait()
-    parts = [st_ref[me]] + [got[d] for d in range(1, n)]
-    m = functools.reduce(jnp.maximum, [p[0:1] for p in parts])
-    total = sum(p[1:2] * jnp.exp(p[0:1] - m) for p in parts)
-    target = sum(p[2:3] for p in parts)
-    w = mask_ref[me]
-    scale = w / count
-    term = w * (jnp.log(total) + m - target)
-    mine = jnp.concatenate([m, scale / total, scale, term, jnp.zeros((4, m.shape[1]), F32)], axis=0)
-    every[me] = mine
-    second = []
-    for d in range(1, n):
-        second.append(pltpu.make_async_remote_copy(
+    second = [
+        pltpu.make_async_remote_copy(
             src_ref=every.at[me], dst_ref=every.at[me], send_sem=send2.at[d], recv_sem=recv2.at[d],
-            device_id={'stage': peers[d]}, device_id_type=MESH))
-        second[-1].start()
+            device_id={'stage': peers[d]}, device_id_type=MESH)
+        for d in range(1, n)
+    ]
+
+    def reduce_stats():
+        for copy in first:
+            copy.wait()
+        parts = [st_ref[me]] + [got[d] for d in range(1, n)]
+        m = functools.reduce(jnp.maximum, [p[0:1] for p in parts])
+        total = sum(p[1:2] * jnp.exp(p[0:1] - m) for p in parts)
+        target = sum(p[2:3] for p in parts)
+        w = mask_ref[me]
+        scale = w / count
+        term = w * (jnp.log(total) + m - target)
+        every[me] = jnp.concatenate([m, scale / total, scale, term, jnp.zeros((4, m.shape[1]), F32)], axis=0)
+
+    loads[1].wait()
+    loads[2].wait()
+    tiles = y_hbm.shape[1] // MLP_TILE
+
+    def piece(q, carry):
+        m, i = q // layers, lax.rem(q, layers)
+        slot = lax.rem(m, 2)
+
+        @pl.when(i == 0)
+        def _():
+            @pl.when(m < tiles - 1)
+            def _():
+                load_a(m + 1).start()
+
+            load_a(m).wait()
+
+            @pl.when(m >= 2)
+            def _():
+                store_y(m - 2).wait()
+
+            y_buf[slot] = a_buf[slot]
+
+        @pl.when(is_middle())
+        def _():
+            y_buf[slot] = mlp_layer(y_buf[slot], upt_buf.at[i], down_buf.at[i])
+
+        @pl.when(i == layers - 1)
+        def _():
+            store_y(m).start()
+
+        @pl.when(q == 1)
+        def _():
+            for way in range(2):
+                forward(way, 0, way)
+            reduce_stats()
+            for copy in second:
+                copy.start()
+
+        for at, (k, flip) in {2: (1, 1), 3: (1, 0), 4: (2, 1), 6: (2, 0)}.items():
+            @pl.when(q == at)
+            def _():
+                for way in range(2):
+                    forward(way, k, 1 - way if flip else way)
+        return carry
+
+    lax.fori_loop(0, tiles * layers, piece, 0)
     for copy in second:
         copy.wait()
     out_ref[...] = every[...]
     loss_ref[...] = jnp.broadcast_to(jnp.sum(every[:, 3, :], keepdims=True) / count, loss_ref.shape)
-
-
-def stats(st, mask):
+    for h in range(2):
+        for way in range(2):
+            unit(way, far - 1, h, own.at[0]).wait_recv()
+    total = own[here.z].astype(F32) + (chain[far - 1].astype(F32) + chain[2 * far - 1].astype(F32))
+    h_ref[...] = total.astype(BF16)
+    for way in range(2):
+        for k in range(far):
+            for h in range(2):
+                if k > 0 or h == way:
+                    unit(way, k, h, own.at[0]).wait_send()
+    for m in range(tiles - 2, tiles):
+        store_y(m).wait()
+
+
+def stats(st, mask, hsum, at, upt, down):
     n, _, tok = st.shape
+    chips, dim, _ = hsum.shape
+    tokens = MLP_STATS * MLP_TILE
     vmem = pl.BlockSpec(memory_space=pltpu.VMEM)
+    anywhere = pl.BlockSpec(memory_space=pl.ANY)
+    dma = pltpu.SemaphoreType.DMA
     return pl.pallas_call(
         functools.partial(stats_kernel, n),
-        in_specs=[vmem, vmem],
-        out_specs=[vmem, vmem],
-        out_shape=[jax.ShapeDtypeStruct((n, 8, tok), F32), jax.ShapeDtypeStruct((8, 128), F32)],
+        in_specs=[vmem, vmem] + [anywhere] * 4,
+        out_specs=[vmem, vmem, vmem, anywhere],
+        out_shape=[
+            jax.ShapeDtypeStruct((n, 8, tok), F32),
+            jax.ShapeDtypeStruct((8, 128), F32),
+            jax.ShapeDtypeStruct((dim, tok), BF16),
+            jax.ShapeDtypeStruct((dim, tokens), BF16),
+        ],
         scratch_shapes=[
             pltpu.VMEM((n, 8, tok), F32),
             pltpu.VMEM((n, 8, tok), F32),
-        ] + [pltpu.SemaphoreType.DMA((n,))] * 4,
-        compiler_params=params(16, collective_id=0, has_side_effects=True),
-        cost_estimate=cost(1e9, 2e6),
+            pltpu.VMEM((chips, dim, tok), BF16),
+            pltpu.VMEM((chips, dim, tok), BF16),
+            pltpu.VMEM(upt.shape, BF16),
+            pltpu.VMEM(down.shape, BF16),
+            pltpu.VMEM((2, dim, MLP_TILE), BF16),
+            pltpu.VMEM((2, dim, MLP_TILE), BF16),
+            dma((n,)), dma((n,)), dma((n,)), dma((n,)), dma((3,)), dma((16,)), dma((16,)), dma((2,)), dma((2,)),
+        ],
+        compiler_params=params(56, collective_id=0, has_side_effects=True),
+        cost_estimate=cost(3e10, 2e7),
         name='stats',
-    )(st, mask)
+    )(st, mask, hsum, at, upt, down)
 
 
 def grad_kernel(n, e_hbm, w_hbm, x_hbm, a_hbm, upt_hbm, down_hbm, cm_ref, gs_ref, lab_ref, dx_ref, dw_hbm, y_hbm, g_buf, send_buf,
@@ -373,7 +628,7 @@
 
         def load_a(m):
             slot = lax.rem(m, 2)
-            return pltpu.make_async_copy(a_hbm.at[:, cols(m + MLP_FIRST)], a_buf.at[slot], a_sem.at[slot])
+            return pltpu.make_async_copy(a_hbm.at[:, cols(m + MLP_GATHER + MLP_STATS)], a_buf.at[slot], a_sem.at[slot])
 
         def store_y(m):
             slot = lax.rem(m, 2)
@@ -437,7 +692,10 @@
 
             @pl.when(is_middle())
             def _():
-                y_buf[slot] = mlp_layers(a_buf[slot], upt_buf, down_buf)
+                h = a_buf[slot]
+                for i in range(upt_buf.shape[0]):
+                    h = mlp_layer(h, upt_buf.at[i], down_buf.at[i])
+                y_buf[slot] = h
 
             @pl.when(jnp.logical_not(is_middle()))
             def _():
@@ -475,7 +733,7 @@
     dim, rows = wt.shape
     n, _, tok = e.shape
     chips = n // 2
-    tokens = at.shape[1] - MLP_FIRST * MLP_TILE
+    tokens = at.shape[1] - (MLP_GATHER + MLP_STATS) * MLP_TILE
     vmem = pl.BlockSpec(memory_space=pltpu.VMEM)
     anywhere = pl.BlockSpec(memory_space=pl.ANY)
     dma = pltpu.SemaphoreType.DMA
@@ -512,20 +770,15 @@
     def per_device(x_loc, w_loc, labels, loss_mask, e_loc, next_ids, acts_loc, up_loc, down_loc):
         tok = x_loc.shape[0]
         offset = lax.axis_index('stage') * w_loc.shape[0]
-        wt = w_loc.T
-        x = lax.all_gather(x_loc.T, 'stage', axis=0)
+        wt, at, down = w_loc.T, acts_loc[0].T, jnp.swapaxes(down_loc[0], 1, 2)
         ids = (next_ids - offset).reshape(n, 1, tok)
         lab = (labels - offset).reshape(n, 1, tok)
         mask = loss_mask.astype(F32).reshape(n, 1, tok)
-        embed_part = embed(ids, e_loc.T)
-        embed_rows = lax.psum_scatter(embed_part, 'stage', scatter_dimension=0)
-        at, down = acts_loc[0].T, jnp.swapaxes(down_loc[0], 1, 2)
-        y0, upt = mlp(at, up_loc[0], down)
-        lab, y0 = lax.optimization_barrier((lab, y0))
+        x, hsum, y0, upt = gather(x_loc.T, ids, e_loc.T, up_loc[0], down, at)
         e, cm, st = logits(wt, x, lab)
-        gs, loss = stats(st, mask)
-        dx, dw, y1 = grad(wt, e, x, at, upt, down, cm, gs, lab)
-        stage_out = jnp.concatenate([y0, y1], axis=1)
+        gs, loss, embed_rows, y1 = stats(st, mask, hsum, at, upt, down)
+        dx, dw, y2 = grad(wt, e, x, at, upt, down, cm, gs, lab)
+        stage_out = jnp.concatenate([y0, y1, y2], axis=1)
         return loss[0, :1], dx.T, dw.T, embed_rows.T, stage_out.T[None]
 
     return jax.shard_map(

time: 202 us -> 191 us (0.946)
  between operations: 14.1 us -> 0.7 us
  Pallas kernels: 169 us -> 179 us
  local copies, waits for them, and re-layouts: 11.1 us -> 4.54 us
    pallas_call x3 -> x2, Pallas kernels: 64.8 us -> 80.7 us  [the longest x1 40.6 us: stats(): pl.pallas_call(functools.partial(stats_kernel, n), in_specs=[vmem, vmem]...]
    unnamed x16 -> x13, local copies, waits for them, and re-layouts: 10.6 us -> 3.34 us
    pallas_call x1, Pallas kernels: 69.2 us -> 63.2 us  [grad(): pl.pallas_call(functools.partial(grad_kernel, n), in_specs=[anywhere] * 6...]
  transfers between devices with their start and end apart: 2 -> 0, of which waited for: 0 -> 0; matrix products, arithmetic and copies ran while one was open for 4% -> 0% of each run, Pallas kernels for 84% -> 0%
where the time goes in v4:
time: 191 us
  Pallas kernels  179 us (94%)
  other arithmetic  6.09 us (3%)
  local copies, waits for them, and re-layouts  4.54 us (2%)
    pallas_call x1, Pallas kernels, grad(): pl.pallas_call(functools.partial(grad_kernel, n), in_specs=[anywhere] * 6...  63.2 us
    pallas_call x1, Pallas kernels, stats(): pl.pallas_call(functools.partial(stats_kernel, n), in_specs=[vmem, vmem]...  40.6 us
    pallas_call x1, Pallas kernels, gather(): pl.pallas_call(functools.partial(gather_kernel, n), in_specs=[vmem, vmem]...  40.1 us
    pallas_call x1, Pallas kernels, logits(): pl.pallas_call(logits_kernel, grid=(n // GROUP,), in_specs=[pl.BlockSpec(...  35.4 us
    broadcast_in_dim x1, other arithmetic, per_device(): return (loss[0, :1], dx.T, dw.T, embed_rows.T, stage_out.T[None])  4.14 us

profile of v4, /device:TPU:21, one launch (start us, length us, event | category | flops | bytes accessed | tf_op | source)
XLA Modules:
  0.0 190.6 jit_solution(6210971168077119324)
XLA Ops:
  0.6 1.4 broadcast_subtract_fusion
  2.0 40.1 %gather.1 = (bf16[16,576,256]{2,1,0:T(8,128)(2,1)}, bf16[8,576,256]{2,1,0:T(8,128)(2,1)}, bf16[576,512]{1,0:T(8,128)(2,1)}, bf16[2,1536,576]{2,1,0:T(8,128)(2,1)}) custom-call(bf16[576,256]{1,0:T(8,128)(2,1)} %bitcast.38, s32[16,1,256]{2,1,0:T(1,128)} %bitcast.27, bf16[576,3072]{1,0:T(8,128)(2,1)} %bitcast.31, bf16[2,576,1536]{2,1,0:T(8,128)(2,1)} %bitcast.32, ...), custom_call_target="tpu_custom_call" | custom-call | flops 14495514624 | bytes 9437184 | tf_op jit(solution)/shard_map/gather/pallas_call | solution.py:226
  42.1 0.0 copy-start.4
  42.1 35.4 %logits.1 = (f32[16,3072,256]{2,1,0:T(8,128)}, f32[16,8,256]{2,1,0:T(8,128)}, f32[16,8,256]{2,1,0:T(8,128)}) custom-call(bf16[576,3072]{1,0:T(8,128)(2,1)} %bitcast.33, bf16[16,576,256]{2,1,0:T(8,128)(2,1)} %get-tuple-element.19.x_ref.x_hbm, s32[16,1,256]{2,1,0:T(1,128)} %bitcast.25), custom_call_target="tpu_custom_call" | custom-call | flops 14495514624 | bytes 50331648 | tf_op jit(solution)/shard_map/logits/pallas_call | solution.py:291
  77.4 0.0 copy-done.4
  77.5 0.6 convert_element_type.3
  78.1 40.6 %stats.1 = (f32[16,8,256]{2,1,0:T(8,128)}, f32[8,128]{1,0:T(8,128)}, bf16[576,256]{1,0:T(8,128)(2,1)}, bf16[576,2560]{1,0:T(8,128)(2,1)}) custom-call(f32[16,8,256]{2,1,0:T(8,128)} %get-tuple-element.20.st_ref, f32[16,1,256]{2,1,0:T(1,128)} %bitcast.24, bf16[8,576,256]{2,1,0:T(8,128)(2,1)} %get-tuple-element.21.h_hbm, bf16[576,4096]{1,0:T(8,128)(2,1)} %bitcast.29, ...), custom_call_target="tpu_custom_call" | custom-call | flops 30000001024 | bytes 20000000 | tf_op jit(solution)/shard_map/stats/pallas_call | solution.py:462
  118.7 1.2 slice.3
  119.9 0.0 copy-start.1
  119.9 63.2 %grad.1 = (f32[576,256]{1,0:T(8,128)}, bf16[576,3072]{1,0:T(8,128)(2,1)}, bf16[576,1024]{1,0:T(8,128)(2,1)}) custom-call(f32[16,3072,256]{2,1,0:T(8,128)} %get-tuple-element.24.e_hbm, bf16[576,3072]{1,0:T(8,128)(2,1)} %bitcast.34, bf16[16,576,256]{2,1,0:T(8,128)(2,1)} %get-tuple-element.19.x_ref.x_hbm, bf16[576,4096]{1,0:T(8,128)(2,1)} %bitcast.30, ...), custom_call_target="tpu_custom_call" | custom-call | flops 43486543872 | bytes 75497472 | tf_op jit(solution)/shard_map/grad/pallas_call | solution.py:740
  183.1 0.0 copy-done.1
  183.1 0.0 copy-start.2
  183.1 0.0 copy-start
  183.1 4.1 %maximum_bitcast_fusion = bf16[1,4096,576]{1,2,0:T(8,128)(2,1)} fusion(bf16[576,1024]{1,0:T(8,128)(2,1)} %get-tuple-element.32, bf16[576,2560]{1,0:T(8,128)(2,1)} %get-tuple-element.31, bf16[576,512]{1,0:T(8,128)(2,1)S(1)} %copy-done.1), kind=kLoop, calls=%fused_computation | loop fusion | flops 14155776 | bytes 9437184 | tf_op jit(solution)/shard_map/broadcast_in_dim | solution.py:782
  187.2 0.0 copy-done.2
  187.2 0.0 copy-start.3
  187.3 0.8 copy.17
  188.1 0.0 copy-done
  188.1 1.8 copy.18
  189.9 0.0 copy-done.3
  189.9 0.7 copy.19
Async XLA Ops:
  42.1 35.4 %copy-start.4 = (s32[4096]{0:T(1024)S(1)}, s32[4096]{0:T(1024)}, u32[]{:S(2)}) copy-start(s32[4096]{0:T(1024)} %param.12) | copy-start | bytes 49156
  119.9 63.2 %copy-start.1 = (bf16[576,512]{1,0:T(8,128)(2,1)S(1)}, bf16[576,512]{1,0:T(8,128)(2,1)}, u32[]{:S(2)}) copy-start(bf16[576,512]{1,0:T(8,128)(2,1)} %get-tuple-element.30) | copy-start | bytes 1769476
  183.1 4.2 %copy-start.2 = (f32[576,256]{1,0:T(8,128)S(1)}, f32[576,256]{1,0:T(8,128)}, u32[]{:S(2)}) copy-start(f32[576,256]{1,0:T(8,128)} %get-tuple-element.27) | copy-start | bytes 1769476
  183.1 5.0 %copy-start = (bf16[576,3072]{1,0:T(8,128)(2,1)S(1)}, bf16[576,3072]{1,0:T(8,128)(2,1)}, u32[]{:S(2)}) copy-start(bf16[576,3072]{1,0:T(8,128)(2,1)} %get-tuple-element.28) | copy-start | bytes 10616836
  187.2 2.6 %copy-start.3 = (bf16[576,256]{1,0:T(8,128)(2,1)S(1)}, bf16[576,256]{1,0:T(8,128)(2,1)}, u32[]{:S(2)}) copy-start(bf16[576,256]{1,0:T(8,128)(2,1)} %get-tuple-element.29) | copy-start | bytes 884740

commit v5 on v4

--- a/solution.py
+++ b/solution.py
@@ -44,8 +44,8 @@
 
 
 MLP_TILE = 512
-MLP_GATHER = 1
-MLP_STATS = 5
+MLP_GATHER = 2
+MLP_STATS = 3
 
 
 def mlp_layer(h, upt, down):
@@ -58,16 +58,6 @@
 def is_middle():
     stage = lax.axis_index('stage')
     return (stage > 0) & (stage < lax.axis_size('stage') - 1)
-
-
-def mlp_step(src, dst, upt, down):
-    @pl.when(is_middle())
-    def _():
-        dst[...] = mlp_layer(src[...], upt, down)
-
-    @pl.when(jnp.logical_not(is_middle()))
-    def _():
-        dst[...] = src[...]
 
 
 class Place:
@@ -103,7 +93,7 @@
     loads = [
         pltpu.make_async_copy(src, dst, load_sem.at[k])
         for k, (src, dst) in enumerate([
-            (et_hbm, et), (up_hbm, up_buf), (down_hbm, down_buf), (a_hbm.at[:, pl.ds(0, MLP_TILE)], a_buf), (x_ref, x_all.at[mine])])
+            (et_hbm, et), (up_hbm, up_buf), (down_hbm, down_buf), (a_hbm.at[:, pl.ds(0, MLP_GATHER * MLP_TILE)], a_buf), (x_ref, x_all.at[mine])])
     ]
     for load in loads:
         load.start()
@@ -187,7 +177,22 @@
         transpose_into(upt_buf.at[i], up_buf[i], 256)
     loads[2].wait()
     loads[3].wait()
-    mlp_step(a_buf, y_buf, upt_buf.at[0], down_buf.at[0])
+    def tiles(m, carry):
+        cols = pl.ds(pl.multiple_of(m * MLP_TILE, MLP_TILE), MLP_TILE)
+
+        @pl.when(is_middle())
+        def _():
+            h = a_buf[:, cols]
+            for i in range(layers):
+                h = mlp_layer(h, upt_buf.at[i], down_buf.at[i])
+            y_buf[:, cols] = h
+
+        @pl.when(jnp.logical_not(is_middle()))
+        def _():
+            y_buf[:, cols] = a_buf[:, cols]
+        return carry
+
+    lax.fori_loop(0, 1, tiles, 0)
     event(here.chips - 2)
     pair_add(here.chips - 1)
     outs = [
@@ -202,8 +207,7 @@
         for k, h in arrivals[way]:
             side(way, k, h).wait()
     outs[2].start()
-    for i in range(1, layers):
-        mlp_step(y_buf, y_buf, upt_buf.at[i], down_buf.at[i])
+    lax.fori_loop(1, MLP_GATHER, tiles, 0)
     outs[3].start()
     for way in range(2):
         for k, h in arrivals[way]:
@@ -252,7 +256,35 @@
     )(xt, ids, et, up, down, at)
 
 
-def logits_kernel(wt_ref, x_ref, lab_ref, e_ref, cm_ref, st_ref, w_ref):
+def logits_kernel(n, wt_ref, x_ref, lab_ref, h_hbm, e_ref, cm_ref, st_ref, h_ref, w_ref, own, chain, load_sem, chain_send, chain_recv):
+    here = Place(n)
+    far = here.far
+    half = h_ref.shape[0] // 2
+    step = pl.program_id(0)
+    load = pltpu.make_async_copy(h_hbm, own, load_sem.at[0])
+
+    @pl.when(step == 0)
+    def _():
+        load.start()
+        here.greet(pltpu.get_barrier_semaphore())
+
+    def target_chip(way, k):
+        return here.chip(far - k if way == 0 else k - far)
+
+    def unit(way, k, h, src):
+        sl = pl.ds(h * half, half)
+        s = way * 8 + k * 2 + h
+        return pltpu.make_async_remote_copy(
+            src_ref=src.at[sl, :], dst_ref=chain.at[way * far + k, sl, :], send_sem=chain_send.at[s], recv_sem=chain_recv.at[s],
+            device_id=here.along[way], device_id_type=MESH)
+
+    def forward(way, k, h):
+        arrived = chain.at[way * far + k]
+        unit(way, k, h, arrived).wait_recv()
+        sl = pl.ds(h * half, half)
+        arrived[sl, :] = (arrived[sl, :].astype(F32) + own[target_chip(way, k + 1), sl, :].astype(F32)).astype(BF16)
+        unit(way, k + 1, h, arrived).start()
+
     rows = wt_ref.shape[1]
     tok = x_ref.shape[2]
 
@@ -283,39 +315,81 @@
         cm_ref[b] = cm[:, b * tok:(b + 1) * tok]
         st_ref[b] = st[:, b * tok:(b + 1) * tok]
 
-
-def logits(wt, x, lab):
+    @pl.when(step == 0)
+    def _():
+        load.wait()
+        for way in range(2):
+            unit(way, 0, way, own.at[target_chip(way, 0)]).start()
+        for way in range(2):
+            unit(way, 1, 1 - way, own.at[target_chip(way, 1)]).start()
+
+    @pl.when(step == 2)
+    def _():
+        for way in range(2):
+            forward(way, 0, way)
+        for way in range(2):
+            forward(way, 1, 1 - way)
+
+    @pl.when(step == 4)
+    def _():
+        for way in range(2):
+            forward(way, 1, way)
+        for way in range(2):
+            forward(way, 2, 1 - way)
+
+    @pl.when(step == 6)
+    def _():
+        for way in range(2):
+            forward(way, 2, way)
+
+    @pl.when(step == 7)
+    def _():
+        for h in range(2):
+            for way in range(2):
+                unit(way, far - 1, h, own.at[0]).wait_recv()
+        total = own[here.z].astype(F32) + (chain[far - 1].astype(F32) + chain[2 * far - 1].astype(F32))
+        h_ref[...] = total.astype(BF16)
+        for way in range(2):
+            for k in range(far):
+                for h in range(2):
+                    if k > 0 or h == way:
+                        unit(way, k, h, own.at[0]).wait_send()
+
+
+def logits(wt, x, lab, hsum):
     dim, rows = wt.shape
     n, _, tok = x.shape
     block = lambda r, c: pl.BlockSpec((GROUP, r, c), lambda i: (i, 0, 0))
+    dma = pltpu.SemaphoreType.DMA
     return pl.pallas_call(
-        logits_kernel,
+        functools.partial(logits_kernel, n),
         grid=(n // GROUP,),
-        in_specs=[pl.BlockSpec((dim, rows), lambda i: (0, 0)), block(dim, tok), block(1, tok)],
-        out_specs=[block(rows, tok), block(8, tok), block(8, tok)],
+        in_specs=[
+            pl.BlockSpec((dim, rows), lambda i: (0, 0)), block(dim, tok), block(1, tok), pl.BlockSpec(memory_space=pl.ANY)],
+        out_specs=[block(rows, tok), block(8, tok), block(8, tok), pl.BlockSpec((dim, tok), lambda i: (0, 0))],
         out_shape=[
             jax.ShapeDtypeStruct((n, rows, tok), F32),
             jax.ShapeDtypeStruct((n, 8, tok), F32),
             jax.ShapeDtypeStruct((n, 8, tok), F32),
+            jax.ShapeDtypeStruct((dim, tok), BF16),
         ],
-        scratch_shapes=[pltpu.VMEM((rows, dim), BF16)],
-        compiler_params=params(56),
+        scratch_shapes=[
+            pltpu.VMEM((rows, dim), BF16), pltpu.VMEM(hsum.shape, BF16), pltpu.VMEM(hsum.shape, BF16),
+            dma((1,)), dma((16,)), dma((16,)),
+        ],
+        compiler_params=params(56, collective_id=3, has_side_effects=True),
         cost_estimate=cost(2 * n * tok * dim * rows, 4 * n * tok * rows),
         name='logits',
-    )(wt, x, lab)
-
-
-def stats_kernel(n, st_ref, mask_ref, h_hbm, a_hbm, upt_hbm, down_hbm, out_ref, loss_ref, h_ref, y_hbm, got, every, own, chain,
-                 upt_buf, down_buf, a_buf, y_buf, send1, recv1, send2, recv2, load_sem, chain_send, chain_recv, a_sem, y_sem):
-    here = Place(n)
+    )(wt, x, lab, hsum)
+
+
+def stats_kernel(n, st_ref, mask_ref, a_hbm, upt_hbm, down_hbm, out_ref, loss_ref, y_hbm, got, every, upt_buf, down_buf, a_buf,
+                 y_buf, send1, recv1, send2, recv2, load_sem, a_sem, y_sem):
     me = lax.axis_index('stage')
-    dim = h_ref.shape[0]
-    half = dim // 2
-    far = here.far
     layers = upt_buf.shape[0]
     loads = [
         pltpu.make_async_copy(src, dst, load_sem.at[k])
-        for k, (src, dst) in enumerate([(h_hbm, own), (upt_hbm, upt_buf), (down_hbm, down_buf)])
+        for k, (src, dst) in enumerate([(upt_hbm, upt_buf), (down_hbm, down_buf)])
     ]
     for load in loads:
         load.start()
@@ -343,29 +417,6 @@
             src_ref=st_ref.at[peers[d]], dst_ref=got.at[d], send_sem=send1.at[d], recv_sem=recv1.at[d],
             device_id={'stage': peers[d]}, device_id_type=MESH))
         first[-1].start()
-
-    def target_chip(way, k):
-        return here.chip(far - k if way == 0 else k - far)
-
-    def unit(way, k, h, src):
-        sl = pl.ds(h * half, half)
-        s = way * 8 + k * 2 + h
-        return pltpu.make_async_remote_copy(
-            src_ref=src.at[sl, :], dst_ref=chain.at[way * far + k, sl, :], send_sem=chain_send.at[s], recv_sem=chain_recv.at[s],
-            device_id=here.along[way], device_id_type=MESH)
-
-    def forward(way, k, h):
-        arrived = chain.at[way * far + k]
-        unit(way, k, h, arrived).wait_recv()
-        sl = pl.ds(h * half, half)
-        arrived[sl, :] = (arrived[sl, :].astype(F32) + own[target_chip(way, k + 1), sl, :].astype(F32)).astype(BF16)
-        unit(way, k + 1, h, arrived).start()
-
-    loads[0].wait()
-    for way in range(2):
-        unit(way, 0, way, own.at[target_chip(way, 0)]).start()
-    for way in range(2):
-        unit(way, 1, 1 - way, own.at[target_chip(way, 1)]).start()
 
     weight = mask_ref[...]
     count = jnp.maximum(jnp.sum(weight, keepdims=True)[0], 1.0)
@@ -388,8 +439,8 @@
         term = w * (jnp.log(total) + m - target)
         every[me] = jnp.concatenate([m, scale / total, scale, term, jnp.zeros((4, m.shape[1]), F32)], axis=0)
 
-    loads[1].wait()
-    loads[2].wait()
+    for load in loads:
+        load.wait()
     tiles = y_hbm.shape[1] // MLP_TILE
 
     def piece(q, carry):
@@ -420,17 +471,10 @@
 
         @pl.when(q == 1)
         def _():
-            for way in range(2):
-                forward(way, 0, way)
             reduce_stats()
             for copy in second:
                 copy.start()
 
-        for at, (k, flip) in {2: (1, 1), 3: (1, 0), 4: (2, 1), 6: (2, 0)}.items():
-            @pl.when(q == at)
-            def _():
-                for way in range(2):
-                    forward(way, k, 1 - way if flip else way)
         return carry
 
     lax.fori_loop(0, tiles * layers, piece, 0)
@@ -438,52 +482,39 @@
         copy.wait()
     out_ref[...] = every[...]
     loss_ref[...] = jnp.broadcast_to(jnp.sum(every[:, 3, :], keepdims=True) / count, loss_ref.shape)
-    for h in range(2):
-        for way in range(2):
-            unit(way, far - 1, h, own.at[0]).wait_recv()
-    total = own[here.z].astype(F32) + (chain[far - 1].astype(F32) + chain[2 * far - 1].astype(F32))
-    h_ref[...] = total.astype(BF16)
-    for way in range(2):
-        for k in range(far):
-            for h in range(2):
-                if k > 0 or h == way:
-                    unit(way, k, h, own.at[0]).wait_send()
     for m in range(tiles - 2, tiles):
         store_y(m).wait()
 
 
-def stats(st, mask, hsum, at, upt, down):
+def stats(st, mask, at, upt, down):
     n, _, tok = st.shape
-    chips, dim, _ = hsum.shape
+    dim = at.shape[0]
     tokens = MLP_STATS * MLP_TILE
     vmem = pl.BlockSpec(memory_space=pltpu.VMEM)
     anywhere = pl.BlockSpec(memory_space=pl.ANY)
     dma = pltpu.SemaphoreType.DMA
     return pl.pallas_call(
         functools.partial(stats_kernel, n),
-        in_specs=[vmem, vmem] + [anywhere] * 4,
-        out_specs=[vmem, vmem, vmem, anywhere],
+        in_specs=[vmem, vmem] + [anywhere] * 3,
+        out_specs=[vmem, vmem, anywhere],
         out_shape=[
             jax.ShapeDtypeStruct((n, 8, tok), F32),
             jax.ShapeDtypeStruct((8, 128), F32),
-            jax.ShapeDtypeStruct((dim, tok), BF16),
             jax.ShapeDtypeStruct((dim, tokens), BF16),
         ],
         scratch_shapes=[
             pltpu.VMEM((n, 8, tok), F32),
             pltpu.VMEM((n, 8, tok), F32),
-            pltpu.VMEM((chips, dim, tok), BF16),
-            pltpu.VMEM((chips, dim, tok), BF16),
             pltpu.VMEM(upt.shape, BF16),
             pltpu.VMEM(down.shape, BF16),
             pltpu.VMEM((2, dim, MLP_TILE), BF16),
             pltpu.VMEM((2, dim, MLP_TILE), BF16),
-            dma((n,)), dma((n,)), dma((n,)), dma((n,)), dma((3,)), dma((16,)), dma((16,)), dma((2,)), dma((2,)),
+            dma((n,)), dma((n,)), dma((n,)), dma((n,)), dma((2,)), dma((2,)), dma((2,)),
         ],
         compiler_params=params(56, collective_id=0, has_side_effects=True),
         cost_estimate=cost(3e10, 2e7),
         name='stats',
-    )(st, mask, hsum, at, upt, down)
+    )(st, mask, at, upt, down)
 
 
 def grad_kernel(n, e_hbm, w_hbm, x_hbm, a_hbm, upt_hbm, down_hbm, cm_ref, gs_ref, lab_ref, dx_ref, dw_hbm, y_hbm, g_buf, send_buf,
@@ -507,11 +538,6 @@
     def block_at(i, own_side):
         return 2 * chip_at(i) + (core if own_side else 1 - core)
 
-    barrier = pltpu.get_barrier_semaphore()
-    for peer in (partner, ahead, behind):
-        pl.semaphore_signal(barrier, inc=1, device_id=peer, device_id_type=MESH)
-    pl.semaphore_wait(barrier, 3)
-
     def pair_copy(i):
         return pltpu.make_async_remote_copy(
             src_ref=send_buf.at[lax.rem(i, 2)], dst_ref=pair.at[i], send_sem=pair_send.at[lax.rem(i, 2)],
@@ -553,6 +579,10 @@
             load_e(0, q).start()
         load_w = pltpu.make_async_copy(w_hbm, w_buf, load_sem.at[0])
         load_w.start()
+        barrier = pltpu.get_barrier_semaphore()
+        for peer in (partner, ahead, behind):
+            pl.semaphore_signal(barrier, inc=1, device_id=peer, device_id_type=MESH)
+        pl.semaphore_wait(barrier, 3)
         index = lax.broadcasted_iota(jnp.int32, (CHUNK, tok), 0)
         load_w.wait()
 
@@ -669,6 +699,11 @@
             def _():
                 for way in range(2):
                     forward(way, 2, 1 - way)
+
+            @pl.when(j == pieces - 1)
+            def _():
+                for way in range(2):
+                    forward(way, 2, way)
             return carry
 
         lax.fori_loop(0, pieces, head, 0)
@@ -702,11 +737,6 @@
                 y_buf[slot] = a_buf[slot]
 
             store_y(m).start()
-
-            @pl.when(m == 0)
-            def _():
-                for way in range(2):
-                    forward(way, 2, way)
             return carry
 
         lax.fori_loop(0, tiles, layers, 0)
@@ -775,8 +805,8 @@
         lab = (labels - offset).reshape(n, 1, tok)
         mask = loss_mask.astype(F32).reshape(n, 1, tok)
         x, hsum, y0, upt = gather(x_loc.T, ids, e_loc.T, up_loc[0], down, at)
-        e, cm, st = logits(wt, x, lab)
-        gs, loss, embed_rows, y1 = stats(st, mask, hsum, at, upt, down)
+        e, cm, st, embed_rows = logits(wt, x, lab, hsum)
+        gs, loss, y1 = stats(st, mask, at, upt, down)
         dx, dw, y2 = grad(wt, e, x, at, upt, down, cm, gs, lab)
         stage_out = jnp.concatenate([y0, y1, y2], axis=1)
         return loss[0, :1], dx.T, dw.T, embed_rows.T, stage_out.T[None]

time: 191 us -> 184 us (0.963)
  Pallas kernels: 179 us -> 172 us
    pallas_call x1, Pallas kernels: 40.6 us -> 24.6 us  [stats(): pl.pallas_call(functools.partial(stats_kernel, n), in_specs=[vmem, vmem]...]
    pallas_call x1, Pallas kernels: 40.1 us -> 43.6 us  [gather(): pl.pallas_call(functools.partial(gather_kernel, n), in_specs=[vmem, vmem]...]
    pallas_call x1, Pallas kernels: 35.4 us -> 38.9 us  [logits(): pl.pallas_call(functools.partial(logits_kernel, n), grid=(n // GROUP,), i...]
where the time goes in v5:
time: 184 us; the launch traced here: 183 us
  Pallas kernels  172 us (93%)
  other arithmetic  6.29 us (3%)
  local copies, waits for them, and re-layouts  4.53 us (2%)
    pallas_call x1, Pallas kernels, grad(): pl.pallas_call(functools.partial(grad_kernel, n), in_specs=[anywhere] * 6...  64.8 us
    pallas_call x1, Pallas kernels, gather(): pl.pallas_call(functools.partial(gather_kernel, n), in_specs=[vmem, vmem]...  43.6 us
    pallas_call x1, Pallas kernels, logits(): pl.pallas_call(functools.partial(logits_kernel, n), grid=(n // GROUP,), i...  38.9 us
    pallas_call x1, Pallas kernels, stats(): pl.pallas_call(functools.partial(stats_kernel, n), in_specs=[vmem, vmem]...  24.6 us
    broadcast_in_dim x1, other arithmetic, per_device(): return (loss[0, :1], dx.T, dw.T, embed_rows.T, stage_out.T[None])  4.33 us

profile of v5, /device:TPU:21, one launch (start us, length us, event | category | flops | bytes accessed | tf_op | source)
XLA Modules:
  0.0 183.4 jit_solution(1520624843419937611)
XLA Ops:
  0.6 1.4 broadcast_subtract_fusion
  2.0 43.6 %gather.1 = (bf16[16,576,256]{2,1,0:T(8,128)(2,1)}, bf16[8,576,256]{2,1,0:T(8,128)(2,1)}, bf16[576,1024]{1,0:T(8,128)(2,1)}, bf16[2,1536,576]{2,1,0:T(8,128)(2,1)}) custom-call(bf16[576,256]{1,0:T(8,128)(2,1)} %bitcast.38, s32[16,1,256]{2,1,0:T(1,128)} %bitcast.27, bf16[576,3072]{1,0:T(8,128)(2,1)} %bitcast.31, bf16[2,576,1536]{2,1,0:T(8,128)(2,1)} %bitcast.32, ...), custom_call_target="tpu_custom_call" | custom-call | flops 14495514624 | bytes 9437184 | tf_op jit(solution)/shard_map/gather/pallas_call | solution.py:230
  45.6 0.0 copy-start.3
  45.6 38.9 %logits.1 = (f32[16,3072,256]{2,1,0:T(8,128)}, f32[16,8,256]{2,1,0:T(8,128)}, f32[16,8,256]{2,1,0:T(8,128)}, bf16[576,256]{1,0:T(8,128)(2,1)}) custom-call(bf16[576,3072]{1,0:T(8,128)(2,1)} %bitcast.33, bf16[16,576,256]{2,1,0:T(8,128)(2,1)} %get-tuple-element.19.x_ref.x_hbm, s32[16,1,256]{2,1,0:T(1,128)} %bitcast.25, ...), custom_call_target="tpu_custom_call" | custom-call | flops 14495514624 | bytes 50331648 | tf_op jit(solution)/shard_map/logits/pallas_call | solution.py:364
  84.5 0.0 copy-done.3
  84.5 0.6 convert_element_type.3
  85.1 24.6 %stats.1 = (f32[16,8,256]{2,1,0:T(8,128)}, f32[8,128]{1,0:T(8,128)}, bf16[576,1536]{1,0:T(8,128)(2,1)}) custom-call(f32[16,8,256]{2,1,0:T(8,128)} %get-tuple-element.21.st_ref, f32[16,1,256]{2,1,0:T(1,128)} %bitcast.24, bf16[576,4096]{1,0:T(8,128)(2,1)} %bitcast.29, bf16[2,1536,576]{2,1,0:T(8,128)(2,1)} %get-tuple-element.22.upt_hbm, ...), custom_call_target="tpu_custom_call" | custom-call | flops 30000001024 | bytes 20000000 | tf_op jit(solution)/shard_map/stats/pallas_call | solution.py:496
  109.7 1.2 slice.3
  110.9 64.8 %grad.1 = (f32[576,256]{1,0:T(8,128)}, bf16[576,3072]{1,0:T(8,128)(2,1)}, bf16[576,1536]{1,0:T(8,128)(2,1)}) custom-call(f32[16,3072,256]{2,1,0:T(8,128)} %get-tuple-element.24.e_hbm, bf16[576,3072]{1,0:T(8,128)(2,1)} %bitcast.34, bf16[16,576,256]{2,1,0:T(8,128)(2,1)} %get-tuple-element.19.x_ref.x_hbm, bf16[576,4096]{1,0:T(8,128)(2,1)} %bitcast.30, ...), custom_call_target="tpu_custom_call" | custom-call | flops 43486543872 | bytes 75497472 | tf_op jit(solution)/shard_map/grad/pallas_call | solution.py:770
  175.7 0.0 copy-start.1
  175.7 0.0 copy-start
  175.7 4.3 %maximum_bitcast_fusion = bf16[1,4096,576]{1,2,0:T(8,128)(2,1)} fusion(bf16[576,1536]{1,0:T(8,128)(2,1)} %get-tuple-element.32, bf16[576,1536]{1,0:T(8,128)(2,1)} %get-tuple-element.31, bf16[576,1024]{1,0:T(8,128)(2,1)} %get-tuple-element.30), kind=kLoop, calls=%fused_computation | loop fusion | flops 14155776 | bytes 9437184 | tf_op jit(solution)/shard_map/broadcast_in_dim | solution.py:812
  180.0 0.0 copy-done.1
  180.0 0.0 copy-start.2
  180.0 0.8 copy.17
  180.9 0.0 copy-done
  180.9 1.8 copy.18
  182.7 0.0 copy-done.2
  182.7 0.7 copy.19
Async XLA Ops:
  45.6 38.9 %copy-start.3 = (s32[4096]{0:T(1024)S(1)}, s32[4096]{0:T(1024)}, u32[]{:S(2)}) copy-start(s32[4096]{0:T(1024)} %param.12) | copy-start | bytes 49156
  175.7 4.4 %copy-start.1 = (f32[576,256]{1,0:T(8,128)S(1)}, f32[576,256]{1,0:T(8,128)}, u32[]{:S(2)}) copy-start(f32[576,256]{1,0:T(8,128)} %get-tuple-element.27) | copy-start | bytes 1769476
  175.7 5.2 %copy-start = (bf16[576,3072]{1,0:T(8,128)(2,1)S(1)}, bf16[576,3072]{1,0:T(8,128)(2,1)}, u32[]{:S(2)}) copy-start(bf16[576,3072]{1,0:T(8,128)(2,1)} %get-tuple-element.28) | copy-start | bytes 10616836
  180.0 2.6 %copy-start.2 = (bf16[576,256]{1,0:T(8,128)(2,1)S(1)}, bf16[576,256]{1,0:T(8,128)(2,1)}, u32[]{:S(2)}) copy-start(bf16[576,256]{1,0:T(8,128)(2,1)} %get-tuple-element.29) | copy-start | bytes 884740

commit v6 on v5

--- a/solution.py
+++ b/solution.py
@@ -10,7 +10,7 @@
 F32 = jnp.float32
 BF16 = jnp.bfloat16
 MESH = pl.DeviceIdType.MESH
-CHUNK = 512
+CHUNK = 384
 GROUP = 2
 MIB = 1024 * 1024
 
@@ -75,10 +75,9 @@
     def block(self, chip, own_side):
         return 2 * chip + (self.core if own_side else 1 - self.core)
 
-    def greet(self, barrier):
+    def hail(self, barrier):
         for peer in [self.partner] + self.along:
             pl.semaphore_signal(barrier, inc=1, device_id=peer, device_id_type=MESH)
-        pl.semaphore_wait(barrier, 3)
 
 
 def gather_kernel(n, x_ref, ids_ref, et_hbm, up_hbm, down_hbm, a_hbm, x_out, h_out, y_out, upt_out, x_all, et, up_buf, upt_buf,
@@ -93,11 +92,14 @@
     loads = [
         pltpu.make_async_copy(src, dst, load_sem.at[k])
         for k, (src, dst) in enumerate([
-            (et_hbm, et), (up_hbm, up_buf), (down_hbm, down_buf), (a_hbm.at[:, pl.ds(0, MLP_GATHER * MLP_TILE)], a_buf), (x_ref, x_all.at[mine])])
+            (up_hbm, up_buf), (down_hbm, down_buf), (a_hbm.at[:, pl.ds(0, MLP_GATHER * MLP_TILE)], a_buf), (et_hbm, et),
+            (x_ref, x_all.at[mine])])
     ]
     for load in loads:
         load.start()
-    here.greet(pltpu.get_barrier_semaphore())
+    barrier = pltpu.get_barrier_semaphore()
+    here.hail(barrier)
+    pl.semaphore_wait(barrier, 3)
 
     def unit(way, k, h):
         sl = pl.ds(h * half, half)
@@ -147,6 +149,28 @@
         own[i] = (own[i].astype(F32) + pair[i].astype(F32)).astype(BF16)
 
     loads[0].wait()
+    for i in range(layers):
+        transpose_into(upt_buf.at[i], up_buf[i], 256)
+    loads[1].wait()
+    loads[2].wait()
+    def tiles(m, carry):
+        cols = pl.ds(pl.multiple_of(m * MLP_TILE, MLP_TILE), MLP_TILE)
+
+        @pl.when(is_middle())
+        def _():
+            h = a_buf[:, cols]
+            for i in range(layers):
+                h = mlp_layer(h, upt_buf.at[i], down_buf.at[i])
+            y_buf[:, cols] = h
+
+        @pl.when(jnp.logical_not(is_middle()))
+        def _():
+            y_buf[:, cols] = a_buf[:, cols]
+        return carry
+
+    lax.fori_loop(0, 1, tiles, 0)
+    event(0)
+    loads[3].wait()
     index = lax.broadcasted_iota(jnp.int32, (rows, 2 * tok), 0)
 
     def embed(i, carry):
@@ -165,39 +189,18 @@
         def _():
             pair_add(i - 1)
 
-        for u in range(here.chips - 2):
-            @pl.when(i == u + 2)
-            def _():
-                event(u)
+        for u, at in enumerate([0, 2, 3, 5, 6]):
+            @pl.when(i == at)
+            def _():
+                event(u + 1)
         return carry
 
     lax.fori_loop(0, here.chips, embed, 0)
-    loads[1].wait()
-    for i in range(layers):
-        transpose_into(upt_buf.at[i], up_buf[i], 256)
-    loads[2].wait()
-    loads[3].wait()
-    def tiles(m, carry):
-        cols = pl.ds(pl.multiple_of(m * MLP_TILE, MLP_TILE), MLP_TILE)
-
-        @pl.when(is_middle())
-        def _():
-            h = a_buf[:, cols]
-            for i in range(layers):
-                h = mlp_layer(h, upt_buf.at[i], down_buf.at[i])
-            y_buf[:, cols] = h
-
-        @pl.when(jnp.logical_not(is_middle()))
-        def _():
-            y_buf[:, cols] = a_buf[:, cols]
-        return carry
-
-    lax.fori_loop(0, 1, tiles, 0)
     event(here.chips - 2)
     pair_add(here.chips - 1)
     outs = [
         pltpu.make_async_copy(src, dst, out_sem.at[k])
-        for k, (src, dst) in enumerate([(own, h_out), (upt_buf, upt_out), (x_all, x_out), (y_buf, y_out)])
+        for k, (src, dst) in enumerate([(own, h_out), (upt_buf, upt_out), (x_all, x_out), (y_buf, y_out.at[:, pl.ds(0, MLP_GATHER * MLP_TILE)])])
     ]
     outs[0].start()
     outs[1].start()
@@ -234,7 +237,7 @@
         out_shape=[
             jax.ShapeDtypeStruct((n, dim, tok), BF16),
             jax.ShapeDtypeStruct((n // 2, dim, tok), BF16),
-            jax.ShapeDtypeStruct((dim, tokens), BF16),
+            jax.ShapeDtypeStruct(at.shape, BF16),
             jax.ShapeDtypeStruct((layers, hidden, dim), BF16),
         ],
         scratch_shapes=[
@@ -266,7 +269,7 @@
     @pl.when(step == 0)
     def _():
         load.start()
-        here.greet(pltpu.get_barrier_semaphore())
+        here.hail(pltpu.get_barrier_semaphore())
 
     def target_chip(way, k):
         return here.chip(far - k if way == 0 else k - far)
@@ -309,7 +312,7 @@
         target += jnp.sum(jnp.where(index == lab - c * CHUNK, z, 0.0), axis=0, keepdims=True)
     m = functools.reduce(jnp.maximum, maxes)
     s = sum(si * jnp.exp(mi - m) for mi, si in zip(maxes, sums))
-    cm = jnp.concatenate(maxes + [jnp.zeros((8 - len(maxes), GROUP * tok), F32)], axis=0)
+    cm = jnp.concatenate(maxes, axis=0)
     st = jnp.concatenate([m, s, target, jnp.zeros((5, GROUP * tok), F32)], axis=0)
     for b in range(GROUP):
         cm_ref[b] = cm[:, b * tok:(b + 1) * tok]
@@ -317,6 +320,7 @@
 
     @pl.when(step == 0)
     def _():
+        pl.semaphore_wait(pltpu.get_barrier_semaphore(), 3)
         load.wait()
         for way in range(2):
             unit(way, 0, way, own.at[target_chip(way, 0)]).start()
@@ -383,7 +387,7 @@
     )(wt, x, lab, hsum)
 
 
-def stats_kernel(n, st_ref, mask_ref, a_hbm, upt_hbm, down_hbm, out_ref, loss_ref, y_hbm, got, every, upt_buf, down_buf, a_buf,
+def stats_kernel(n, st_ref, mask_ref, a_hbm, upt_hbm, down_hbm, y_in, out_ref, loss_ref, y_hbm, got, every, upt_buf, down_buf, a_buf,
                  y_buf, send1, recv1, send2, recv2, load_sem, a_sem, y_sem):
     me = lax.axis_index('stage')
     layers = upt_buf.shape[0]
@@ -401,7 +405,7 @@
 
     def store_y(m):
         slot = lax.rem(m, 2)
-        start = pl.multiple_of(m * MLP_TILE, MLP_TILE)
+        start = pl.multiple_of((m + MLP_GATHER) * MLP_TILE, MLP_TILE)
         return pltpu.make_async_copy(y_buf.at[slot], y_hbm.at[:, pl.ds(start, MLP_TILE)], y_sem.at[slot])
 
     load_a(0).start()
@@ -441,7 +445,7 @@
 
     for load in loads:
         load.wait()
-    tiles = y_hbm.shape[1] // MLP_TILE
+    tiles = MLP_STATS
 
     def piece(q, carry):
         m, i = q // layers, lax.rem(q, layers)
@@ -486,21 +490,20 @@
         store_y(m).wait()
 
 
-def stats(st, mask, at, upt, down):
+def stats(st, mask, at, upt, down, y):
     n, _, tok = st.shape
     dim = at.shape[0]
-    tokens = MLP_STATS * MLP_TILE
     vmem = pl.BlockSpec(memory_space=pltpu.VMEM)
     anywhere = pl.BlockSpec(memory_space=pl.ANY)
     dma = pltpu.SemaphoreType.DMA
     return pl.pallas_call(
         functools.partial(stats_kernel, n),
-        in_specs=[vmem, vmem] + [anywhere] * 3,
+        in_specs=[vmem, vmem] + [anywhere] * 4,
         out_specs=[vmem, vmem, anywhere],
         out_shape=[
             jax.ShapeDtypeStruct((n, 8, tok), F32),
             jax.ShapeDtypeStruct((8, 128), F32),
-            jax.ShapeDtypeStruct((dim, tokens), BF16),
+            jax.ShapeDtypeStruct(y.shape, BF16),
         ],
         scratch_shapes=[
             pltpu.VMEM((n, 8, tok), F32),
@@ -511,13 +514,14 @@
             pltpu.VMEM((2, dim, MLP_TILE), BF16),
             dma((n,)), dma((n,)), dma((n,)), dma((n,)), dma((2,)), dma((2,)), dma((2,)),
         ],
+        input_output_aliases={5: 2},
         compiler_params=params(56, collective_id=0, has_side_effects=True),
         cost_estimate=cost(3e10, 2e7),
         name='stats',
-    )(st, mask, at, upt, down)
-
-
-def grad_kernel(n, e_hbm, w_hbm, x_hbm, a_hbm, upt_hbm, down_hbm, cm_ref, gs_ref, lab_ref, dx_ref, dw_hbm, y_hbm, g_buf, send_buf,
+    )(st, mask, at, upt, down, y)
+
+
+def grad_kernel(n, e_hbm, w_hbm, x_hbm, a_hbm, upt_hbm, down_hbm, y_in, cm_ref, gs_ref, lab_ref, dx_ref, dw_hbm, y_hbm, g_buf, send_buf,
                 own, pair, chain, load_sem, e_sem, pair_send, pair_recv, chain_send, chain_recv, a_sem, y_sem):
     stage = lax.axis_index('stage')
     chips = n // 2
@@ -651,18 +655,19 @@
         ]
         for load in loads:
             load.start()
-        tiles = y_hbm.shape[1] // MLP_TILE
+        done = MLP_GATHER + MLP_STATS
+        tiles = y_hbm.shape[1] // MLP_TILE - done
 
         def cols(m):
             return pl.ds(pl.multiple_of(m * MLP_TILE, MLP_TILE), MLP_TILE)
 
         def load_a(m):
             slot = lax.rem(m, 2)
-            return pltpu.make_async_copy(a_hbm.at[:, cols(m + MLP_GATHER + MLP_STATS)], a_buf.at[slot], a_sem.at[slot])
+            return pltpu.make_async_copy(a_hbm.at[:, cols(m + done)], a_buf.at[slot], a_sem.at[slot])
 
         def store_y(m):
             slot = lax.rem(m, 2)
-            return pltpu.make_async_copy(y_buf.at[slot], y_hbm.at[:, cols(m)], y_sem.at[slot])
+            return pltpu.make_async_copy(y_buf.at[slot], y_hbm.at[:, cols(m + done)], y_sem.at[slot])
 
         load_a(0).start()
         loads[0].wait()
@@ -759,22 +764,21 @@
                     unit(way, k, h, own.at[0]).wait_send()
 
 
-def grad(wt, e, x, at, upt, down, cm, gs, lab):
+def grad(wt, e, x, at, upt, down, y, cm, gs, lab):
     dim, rows = wt.shape
     n, _, tok = e.shape
     chips = n // 2
-    tokens = at.shape[1] - (MLP_GATHER + MLP_STATS) * MLP_TILE
     vmem = pl.BlockSpec(memory_space=pltpu.VMEM)
     anywhere = pl.BlockSpec(memory_space=pl.ANY)
     dma = pltpu.SemaphoreType.DMA
     return pl.pallas_call(
         functools.partial(grad_kernel, n),
-        in_specs=[anywhere] * 6 + [vmem] * 3,
+        in_specs=[anywhere] * 7 + [vmem] * 3,
         out_specs=[vmem, anywhere, anywhere],
         out_shape=[
             jax.ShapeDtypeStruct((dim, tok), F32),
             jax.ShapeDtypeStruct((dim, rows), BF16),
-            jax.ShapeDtypeStruct((dim, tokens), BF16),
+            jax.ShapeDtypeStruct(y.shape, BF16),
         ],
         scratch_shapes=[
             pltpu.VMEM((n, rows, tok), BF16),
@@ -784,10 +788,11 @@
             pltpu.VMEM((chips, dim, tok), F32),
             dma((3,)), dma((2, 2)), dma((2,)), dma((chips,)), dma((16,)), dma((16,)), dma((2,)), dma((2,)),
         ],
+        input_output_aliases={6: 2},
         compiler_params=pltpu.CompilerParams(vmem_limit_bytes=63 * MIB, collective_id=1, has_side_effects=True),
         cost_estimate=cost(6 * n * tok * dim * rows, 6 * n * tok * rows),
         name='grad',
-    )(e, wt, x, at, upt, down, cm, gs, lab)
+    )(e, wt, x, at, upt, down, y, cm, gs, lab)
 
 
 def solution(mesh):
@@ -804,11 +809,10 @@
         ids = (next_ids - offset).reshape(n, 1, tok)
         lab = (labels - offset).reshape(n, 1, tok)
         mask = loss_mask.astype(F32).reshape(n, 1, tok)
-        x, hsum, y0, upt = gather(x_loc.T, ids, e_loc.T, up_loc[0], down, at)
+        x, hsum, y, upt = gather(x_loc.T, ids, e_loc.T, up_loc[0], down, at)
         e, cm, st, embed_rows = logits(wt, x, lab, hsum)
-        gs, loss, y1 = stats(st, mask, at, upt, down)
-        dx, dw, y2 = grad(wt, e, x, at, upt, down, cm, gs, lab)
-        stage_out = jnp.concatenate([y0, y1, y2], axis=1)
+        gs, loss, y = stats(st, mask, at, upt, down, y)
+        dx, dw, stage_out = grad(wt, e, x, at, upt, down, y, cm, gs, lab)
         return loss[0, :1], dx.T, dw.T, embed_rows.T, stage_out.T[None]
 
     return jax.shard_map(

time: 184 us -> 182 us (0.989)
  local copies, waits for them, and re-layouts: 4.53 us -> 10.3 us
  other arithmetic: 6.29 us -> 1.96 us
  Pallas kernels: 172 us -> 168 us
    unnamed x11 -> x12, local copies, waits for them, and re-layouts: 3.34 us -> 9.07 us
    broadcast_in_dim x1 -> x0, other arithmetic: 4.33 us -> none  [per_device(): return (loss[0, :1], dx.T, dw.T, embed_rows.T, stage_out.T[None])]
where the time goes in v6:
time: 182 us; the launch traced here: 181 us
  Pallas kernels  168 us (92%)
  local copies, waits for them, and re-layouts  10.3 us (6%)
  other arithmetic  1.96 us (1%)
    pallas_call x1, Pallas kernels, grad(): pl.pallas_call(functools.partial(grad_kernel, n), in_specs=[anywhere] * 7...  63.5 us
    pallas_call x1, Pallas kernels, gather(): pl.pallas_call(functools.partial(gather_kernel, n), in_specs=[vmem, vmem]...  43.1 us
    pallas_call x1, Pallas kernels, logits(): pl.pallas_call(functools.partial(logits_kernel, n), grid=(n // GROUP,), i...  38 us
    pallas_call x1, Pallas kernels, stats(): pl.pallas_call(functools.partial(stats_kernel, n), in_specs=[vmem, vmem]...  23.8 us
    unnamed x12, local copies, waits for them, and re-layouts  9.07 us

profile of v6, /device:TPU:21, one launch (start us, length us, event | category | flops | bytes accessed | tf_op | source)
XLA Modules:
  0.0 181.4 jit_solution(13795913817076523230)
XLA Ops:
  0.6 1.4 broadcast_subtract_fusion
  2.0 43.1 %gather.1 = (bf16[16,576,256]{2,1,0:T(8,128)(2,1)}, bf16[8,576,256]{2,1,0:T(8,128)(2,1)}, bf16[576,4096]{1,0:T(8,128)(2,1)}, bf16[2,1536,576]{2,1,0:T(8,128)(2,1)}) custom-call(bf16[576,256]{1,0:T(8,128)(2,1)} %bitcast.40, s32[16,1,256]{2,1,0:T(1,128)} %bitcast.29, bf16[576,3072]{1,0:T(8,128)(2,1)} %bitcast.33, bf16[2,576,1536]{2,1,0:T(8,128)(2,1)} %bitcast.34, ...), custom_call_target="tpu_custom_call" | custom-call | flops 14495514624 | bytes 9437184 | tf_op jit(solution)/shard_map/gather/pallas_call | solution.py:233
  45.1 0.0 copy-start.1
  45.1 38.0 %logits.1 = (f32[16,3072,256]{2,1,0:T(8,128)}, f32[16,8,256]{2,1,0:T(8,128)}, f32[16,8,256]{2,1,0:T(8,128)}, bf16[576,256]{1,0:T(8,128)(2,1)}) custom-call(bf16[576,3072]{1,0:T(8,128)(2,1)} %bitcast.35, bf16[16,576,256]{2,1,0:T(8,128)(2,1)} %get-tuple-element.19.x_ref.x_hbm, s32[16,1,256]{2,1,0:T(1,128)} %bitcast.27, ...), custom_call_target="tpu_custom_call" | custom-call | flops 14495514624 | bytes 50331648 | tf_op jit(solution)/shard_map/logits/pallas_call | solution.py:368
  83.1 0.0 copy-done.1
  83.1 0.6 convert_element_type.3
  83.7 23.8 %stats.1 = (f32[16,8,256]{2,1,0:T(8,128)}, f32[8,128]{1,0:T(8,128)}, bf16[576,4096]{1,0:T(8,128)(2,1)}) custom-call(f32[16,8,256]{2,1,0:T(8,128)} %get-tuple-element.21.st_ref, f32[16,1,256]{2,1,0:T(1,128)} %bitcast.26, bf16[576,4096]{1,0:T(8,128)(2,1)} %bitcast.31, ...), custom_call_target="tpu_custom_call", output_to_operand_aliasing={{2}: (5, {})} | custom-call | flops 30000001024 | bytes 20000000 | tf_op jit(solution)/shard_map/stats/pallas_call | solution.py:499
  107.6 1.2 slice.3
  108.8 63.5 %grad.1 = (f32[576,256]{1,0:T(8,128)}, bf16[576,3072]{1,0:T(8,128)(2,1)}, bf16[576,4096]{1,0:T(8,128)(2,1)}) custom-call(f32[16,3072,256]{2,1,0:T(8,128)} %get-tuple-element.25.e_hbm, bf16[576,3072]{1,0:T(8,128)(2,1)} %bitcast.36, bf16[16,576,256]{2,1,0:T(8,128)(2,1)} %get-tuple-element.19.x_ref.x_hbm, ...), custom_call_target="tpu_custom_call", output_to_operand_aliasing={{2}: (6, {})} | custom-call | flops 43486543872 | bytes 75497472 | tf_op jit(solution)/shard_map/grad/pallas_call | solution.py:774
  172.3 0.0 copy-start
  172.3 0.0 slice-start
  172.3 2.1 %copy.22 = f32[256,576]{0,1:T(8,128)} copy(f32[256,576]{0,1:T(8,128)} %bitcast.24) | data formatting | bytes 1179648
  174.4 0.0 slice-start.1
  174.4 4.1 %copy.23 = bf16[3072,576]{0,1:T(8,128)(2,1)} copy(bf16[3072,576]{0,1:T(8,128)(2,1)} %bitcast.23) | data formatting | bytes 7077888
  178.4 0.0 copy-done
  178.4 0.7 copy.24
  179.2 0.0 slice-done
  179.2 0.0 slice-done.1
  179.2 2.2 %copy.25 = bf16[1,4096,576]{1,2,0:T(8,128)(2,1)} copy(bf16[1,4096,576]{1,2,0:T(8,128)(2,1)S(1)} %bitcast.22) | data formatting | bytes 9437184
  (1 shorter events, 0.0 us)
Async XLA Ops:
  45.1 38.0 %copy-start.1 = (s32[4096]{0:T(1024)S(1)}, s32[4096]{0:T(1024)}, u32[]{:S(2)}) copy-start(s32[4096]{0:T(1024)} %param.12) | copy-start | bytes 49156
  172.3 6.2 %copy-start = (bf16[576,256]{1,0:T(8,128)(2,1)S(1)}, bf16[576,256]{1,0:T(8,128)(2,1)}, u32[]{:S(2)}) copy-start(bf16[576,256]{1,0:T(8,128)(2,1)} %get-tuple-element.31) | copy-start | bytes 884740
  172.3 6.9 %slice-start = ((s8[4718592]{0:T(1024)(128)(4,1)}), s8[4194304]{0:T(1024)(128)(4,1)S(1)}, s32[]{:S(2)}) async-start(s8[4718592]{0:T(1024)(128)(4,1)} %bitcast.20), calls=%async_computation | async-start | bytes 8388608
  174.4 4.8 %slice-start.1 = ((s8[4718592]{0:T(1024)(128)(4,1)}), s8[524288]{0:T(1024)(128)(4,1)S(1)}, s32[]{:S(2)}) async-start(s8[4718592]{0:T(1024)(128)(4,1)} %bitcast.20), calls=%async_computation.1 | async-start | bytes 1048576

commit v7 on v6

--- a/solution.py
+++ b/solution.py
@@ -200,7 +200,7 @@
     pair_add(here.chips - 1)
     outs = [
         pltpu.make_async_copy(src, dst, out_sem.at[k])
-        for k, (src, dst) in enumerate([(own, h_out), (upt_buf, upt_out), (x_all, x_out), (y_buf, y_out.at[:, pl.ds(0, MLP_GATHER * MLP_TILE)])])
+        for k, (src, dst) in enumerate([(own, h_out), (upt_buf, upt_out), (x_all, x_out), (y_buf, y_out)])
     ]
     outs[0].start()
     outs[1].start()
@@ -237,7 +237,7 @@
         out_shape=[
             jax.ShapeDtypeStruct((n, dim, tok), BF16),
             jax.ShapeDtypeStruct((n // 2, dim, tok), BF16),
-            jax.ShapeDtypeStruct(at.shape, BF16),
+            jax.ShapeDtypeStruct((dim, tokens), BF16),
             jax.ShapeDtypeStruct((layers, hidden, dim), BF16),
         ],
         scratch_shapes=[
@@ -387,7 +387,7 @@
     )(wt, x, lab, hsum)
 
 
-def stats_kernel(n, st_ref, mask_ref, a_hbm, upt_hbm, down_hbm, y_in, out_ref, loss_ref, y_hbm, got, every, upt_buf, down_buf, a_buf,
+def stats_kernel(n, st_ref, mask_ref, a_hbm, upt_hbm, down_hbm, out_ref, loss_ref, y_hbm, got, every, upt_buf, down_buf, a_buf,
                  y_buf, send1, recv1, send2, recv2, load_sem, a_sem, y_sem):
     me = lax.axis_index('stage')
     layers = upt_buf.shape[0]
@@ -405,7 +405,7 @@
 
     def store_y(m):
         slot = lax.rem(m, 2)
-        start = pl.multiple_of((m + MLP_GATHER) * MLP_TILE, MLP_TILE)
+        start = pl.multiple_of(m * MLP_TILE, MLP_TILE)
         return pltpu.make_async_copy(y_buf.at[slot], y_hbm.at[:, pl.ds(start, MLP_TILE)], y_sem.at[slot])
 
     load_a(0).start()
@@ -490,7 +490,7 @@
         store_y(m).wait()
 
 
-def stats(st, mask, at, upt, down, y):
+def stats(st, mask, at, upt, down):
     n, _, tok = st.shape
     dim = at.shape[0]
     vmem = pl.BlockSpec(memory_space=pltpu.VMEM)
@@ -498,12 +498,12 @@
     dma = pltpu.SemaphoreType.DMA
     return pl.pallas_call(
         functools.partial(stats_kernel, n),
-        in_specs=[vmem, vmem] + [anywhere] * 4,
+        in_specs=[vmem, vmem] + [anywhere] * 3,
         out_specs=[vmem, vmem, anywhere],
         out_shape=[
             jax.ShapeDtypeStruct((n, 8, tok), F32),
             jax.ShapeDtypeStruct((8, 128), F32),
-            jax.ShapeDtypeStruct(y.shape, BF16),
+            jax.ShapeDtypeStruct((dim, MLP_STATS * MLP_TILE), BF16),
         ],
         scratch_shapes=[
             pltpu.VMEM((n, 8, tok), F32),
@@ -514,14 +514,13 @@
             pltpu.VMEM((2, dim, MLP_TILE), BF16),
             dma((n,)), dma((n,)), dma((n,)), dma((n,)), dma((2,)), dma((2,)), dma((2,)),
         ],
-        input_output_aliases={5: 2},
         compiler_params=params(56, collective_id=0, has_side_effects=True),
         cost_estimate=cost(3e10, 2e7),
         name='stats',
-    )(st, mask, at, upt, down, y)
-
-
-def grad_kernel(n, e_hbm, w_hbm, x_hbm, a_hbm, upt_hbm, down_hbm, y_in, cm_ref, gs_ref, lab_ref, dx_ref, dw_hbm, y_hbm, g_buf, send_buf,
+    )(st, mask, at, upt, down)
+
+
+def grad_kernel(n, e_hbm, w_hbm, x_hbm, a_hbm, upt_hbm, down_hbm, cm_ref, gs_ref, lab_ref, dx_ref, dw_hbm, y_hbm, g_buf, send_buf,
                 own, pair, chain, load_sem, e_sem, pair_send, pair_recv, chain_send, chain_recv, a_sem, y_sem):
     stage = lax.axis_index('stage')
     chips = n // 2
@@ -656,7 +655,7 @@
         for load in loads:
             load.start()
         done = MLP_GATHER + MLP_STATS
-        tiles = y_hbm.shape[1] // MLP_TILE - done
+        tiles = y_hbm.shape[1] // MLP_TILE
 
         def cols(m):
             return pl.ds(pl.multiple_of(m * MLP_TILE, MLP_TILE), MLP_TILE)
@@ -667,7 +666,7 @@
 
         def store_y(m):
             slot = lax.rem(m, 2)
-            return pltpu.make_async_copy(y_buf.at[slot], y_hbm.at[:, cols(m + done)], y_sem.at[slot])
+            return pltpu.make_async_copy(y_buf.at[slot], y_hbm.at[:, cols(m)], y_sem.at[slot])
 
         load_a(0).start()
         loads[0].wait()
@@ -764,7 +763,7 @@
                     unit(way, k, h, own.at[0]).wait_send()
 
 
-def grad(wt, e, x, at, upt, down, y, cm, gs, lab):
+def grad(wt, e, x, at, upt, down, cm, gs, lab):
     dim, rows = wt.shape
     n, _, tok = e.shape
     chips = n // 2
@@ -773,12 +772,12 @@
     dma = pltpu.SemaphoreType.DMA
     return pl.pallas_call(
         functools.partial(grad_kernel, n),
-        in_specs=[anywhere] * 7 + [vmem] * 3,
+        in_specs=[anywhere] * 6 + [vmem] * 3,
         out_specs=[vmem, anywhere, anywhere],
         out_shape=[
             jax.ShapeDtypeStruct((dim, tok), F32),
             jax.ShapeDtypeStruct((dim, rows), BF16),
-            jax.ShapeDtypeStruct(y.shape, BF16),
+            jax.ShapeDtypeStruct((dim, at.shape[1] - (MLP_GATHER + MLP_STATS) * MLP_TILE), BF16),
         ],
         scratch_shapes=[
             pltpu.VMEM((n, rows, tok), BF16),
@@ -788,11 +787,10 @@
             pltpu.VMEM((chips, dim, tok), F32),
             dma((3,)), dma((2, 2)), dma((2,)), dma((chips,)), dma((16,)), dma((16,)), dma((2,)), dma((2,)),
         ],
-        input_output_aliases={6: 2},
         compiler_params=pltpu.CompilerParams(vmem_limit_bytes=63 * MIB, collective_id=1, has_side_effects=True),
         cost_estimate=cost(6 * n * tok * dim * rows, 6 * n * tok * rows),
         name='grad',
-    )(e, wt, x, at, upt, down, y, cm, gs, lab)
+    )(e, wt, x, at, upt, down, cm, gs, lab)
 
 
 def solution(mesh):
@@ -809,10 +807,11 @@
         ids = (next_ids - offset).reshape(n, 1, tok)
         lab = (labels - offset).reshape(n, 1, tok)
         mask = loss_mask.astype(F32).reshape(n, 1, tok)
-        x, hsum, y, upt = gather(x_loc.T, ids, e_loc.T, up_loc[0], down, at)
+        x, hsum, y0, upt = gather(x_loc.T, ids, e_loc.T, up_loc[0], down, at)
         e, cm, st, embed_rows = logits(wt, x, lab, hsum)
-        gs, loss, y = stats(st, mask, at, upt, down, y)
-        dx, dw, stage_out = grad(wt, e, x, at, upt, down, y, cm, gs, lab)
+        gs, loss, y1 = stats(st, mask, at, upt, down)
+        dx, dw, y2 = grad(wt, e, x, at, upt, down, cm, gs, lab)
+        stage_out = jnp.concatenate([y0, y1, y2], axis=1)
         return loss[0, :1], dx.T, dw.T, embed_rows.T, stage_out.T[None]
 
     return jax.shard_map(

time: 182 us -> 180 us (0.989)
  local copies, waits for them, and re-layouts: 10.3 us -> 4.53 us
  other arithmetic: 1.96 us -> 6.29 us
    unnamed x12 -> x11, local copies, waits for them, and re-layouts: 9.07 us -> 3.34 us
    broadcast_in_dim x0 -> x1, other arithmetic: none -> 4.33 us  [per_device(): return (loss[0, :1], dx.T, dw.T, embed_rows.T, stage_out.T[None])]
where the time goes in v7:
time: 180 us
  Pallas kernels  168 us (93%)
  other arithmetic  6.29 us (3%)
  local copies, waits for them, and re-layouts  4.53 us (3%)
    pallas_call x1, Pallas kernels, grad(): pl.pallas_call(functools.partial(grad_kernel, n), in_specs=[anywhere] * 6...  63.6 us
    pallas_call x1, Pallas kernels, gather(): pl.pallas_call(functools.partial(gather_kernel, n), in_specs=[vmem, vmem]...  43 us
    pallas_call x1, Pallas kernels, logits(): pl.pallas_call(functools.partial(logits_kernel, n), grid=(n // GROUP,), i...  38 us
    pallas_call x1, Pallas kernels, stats(): pl.pallas_call(functools.partial(stats_kernel, n), in_specs=[vmem, vmem]...  23.8 us
    broadcast_in_dim x1, other arithmetic, per_device(): return (loss[0, :1], dx.T, dw.T, embed_rows.T, stage_out.T[None])  4.33 us

profile of v7, /device:TPU:21, one launch (start us, length us, event | category | flops | bytes accessed | tf_op | source)
XLA Modules:
  0.0 180.0 jit_solution(16695515114090615992)
XLA Ops:
  0.6 1.4 broadcast_subtract_fusion
  2.0 43.0 %gather.1 = (bf16[16,576,256]{2,1,0:T(8,128)(2,1)}, bf16[8,576,256]{2,1,0:T(8,128)(2,1)}, bf16[576,1024]{1,0:T(8,128)(2,1)}, bf16[2,1536,576]{2,1,0:T(8,128)(2,1)}) custom-call(bf16[576,256]{1,0:T(8,128)(2,1)} %bitcast.38, s32[16,1,256]{2,1,0:T(1,128)} %bitcast.27, bf16[576,3072]{1,0:T(8,128)(2,1)} %bitcast.31, bf16[2,576,1536]{2,1,0:T(8,128)(2,1)} %bitcast.32, ...), custom_call_target="tpu_custom_call" | custom-call | flops 14495514624 | bytes 9437184 | tf_op jit(solution)/shard_map/gather/pallas_call | solution.py:233
  45.0 0.0 copy-start.3
  45.1 38.0 %logits.1 = (f32[16,3072,256]{2,1,0:T(8,128)}, f32[16,8,256]{2,1,0:T(8,128)}, f32[16,8,256]{2,1,0:T(8,128)}, bf16[576,256]{1,0:T(8,128)(2,1)}) custom-call(bf16[576,3072]{1,0:T(8,128)(2,1)} %bitcast.33, bf16[16,576,256]{2,1,0:T(8,128)(2,1)} %get-tuple-element.19.x_ref.x_hbm, s32[16,1,256]{2,1,0:T(1,128)} %bitcast.25, ...), custom_call_target="tpu_custom_call" | custom-call | flops 14495514624 | bytes 50331648 | tf_op jit(solution)/shard_map/logits/pallas_call | solution.py:368
  83.0 0.0 copy-done.3
  83.0 0.6 convert_element_type.3
  83.7 23.8 %stats.1 = (f32[16,8,256]{2,1,0:T(8,128)}, f32[8,128]{1,0:T(8,128)}, bf16[576,1536]{1,0:T(8,128)(2,1)}) custom-call(f32[16,8,256]{2,1,0:T(8,128)} %get-tuple-element.21.st_ref, f32[16,1,256]{2,1,0:T(1,128)} %bitcast.24, bf16[576,4096]{1,0:T(8,128)(2,1)} %bitcast.29, bf16[2,1536,576]{2,1,0:T(8,128)(2,1)} %get-tuple-element.22.upt_hbm, ...), custom_call_target="tpu_custom_call" | custom-call | flops 30000001024 | bytes 20000000 | tf_op jit(solution)/shard_map/stats/pallas_call | solution.py:499
  107.5 1.2 slice.3
  108.7 63.6 %grad.1 = (f32[576,256]{1,0:T(8,128)}, bf16[576,3072]{1,0:T(8,128)(2,1)}, bf16[576,1536]{1,0:T(8,128)(2,1)}) custom-call(f32[16,3072,256]{2,1,0:T(8,128)} %get-tuple-element.24.e_hbm, bf16[576,3072]{1,0:T(8,128)(2,1)} %bitcast.34, bf16[16,576,256]{2,1,0:T(8,128)(2,1)} %get-tuple-element.19.x_ref.x_hbm, bf16[576,4096]{1,0:T(8,128)(2,1)} %bitcast.30, ...), custom_call_target="tpu_custom_call" | custom-call | flops 43486543872 | bytes 75497472 | tf_op jit(solution)/shard_map/grad/pallas_call | solution.py:773
  172.3 0.0 copy-start.1
  172.3 0.0 copy-start
  172.3 4.3 %maximum_bitcast_fusion = bf16[1,4096,576]{1,2,0:T(8,128)(2,1)} fusion(bf16[576,1536]{1,0:T(8,128)(2,1)} %get-tuple-element.32, bf16[576,1536]{1,0:T(8,128)(2,1)} %get-tuple-element.31, bf16[576,1024]{1,0:T(8,128)(2,1)} %get-tuple-element.30), kind=kLoop, calls=%fused_computation | loop fusion | flops 14155776 | bytes 9437184 | tf_op jit(solution)/shard_map/broadcast_in_dim | solution.py:815
  176.6 0.0 copy-done.1
  176.6 0.0 copy-start.2
  176.6 0.8 copy.17
  177.4 0.0 copy-done
  177.5 1.8 copy.18
  179.2 0.0 copy-done.2
  179.2 0.7 copy.19
Async XLA Ops:
  45.0 38.0 %copy-start.3 = (s32[4096]{0:T(1024)S(1)}, s32[4096]{0:T(1024)}, u32[]{:S(2)}) copy-start(s32[4096]{0:T(1024)} %param.12) | copy-start | bytes 49156
  172.3 4.4 %copy-start.1 = (f32[576,256]{1,0:T(8,128)S(1)}, f32[576,256]{1,0:T(8,128)}, u32[]{:S(2)}) copy-start(f32[576,256]{1,0:T(8,128)} %get-tuple-element.27) | copy-start | bytes 1769476
  172.3 5.2 %copy-start = (bf16[576,3072]{1,0:T(8,128)(2,1)S(1)}, bf16[576,3072]{1,0:T(8,128)(2,1)}, u32[]{:S(2)}) copy-start(bf16[576,3072]{1,0:T(8,128)(2,1)} %get-tuple-element.28) | copy-start | bytes 10616836
  176.6 2.6 %copy-start.2 = (bf16[576,256]{1,0:T(8,128)(2,1)S(1)}, bf16[576,256]{1,0:T(8,128)(2,1)}, u32[]{:S(2)}) copy-start(bf16[576,256]{1,0:T(8,128)(2,1)} %get-tuple-element.29) | copy-start | bytes 884740
